TPU v7x, 32 devices: a whole 2x2x4 slice. The times are simulated.
32 devices in a mesh: gx: 4 (over y, x), gy: 8 (over z, core).
Axes of the slice: x: 2, y: 2, z: 4, core: 2. Of those that a mesh axis runs over, the one named last changes fastest.
Arguments:
- matrix_tiles: float32 [8, 32, 6, 128, 128], P('gx', 'gy'), may hold values from -4 to 4.5, as said below
- tile_codes: int32 [8, 32, 6], P('gx', 'gy'), may hold values from 0 to 8, as said below
- tile_counts: int32 [8, 32], P('gx', 'gy'), may hold values from 1 to 6, as said below
- right_side: float32 [8, 32, 128], P('gx', 'gy'), may hold values from -8 to 8
- initial_guess: float32 [8, 32, 128], P('gx', 'gy'), may hold values from -4 to 4
Outputs:
- solution: float32 [8, 32, 128], P('gx', 'gy')
- residual: float32 [8, 32, 128], P('gx', 'gy')
- hessenberg: float32 [5, 4], replicated
Inputs may be any that keep to these rules, and one draw needn't show every extreme that they name: tile_codes of slot 0 is 4 (the block itself); the codes of one block row are distinct. `tile_counts`: every block row has at least one live slot; some block row has all 6 slots live. `matrix_tiles`: slot 0 of each block row has a diagonal of 2 to 4 added to its entries.
All inputs are finite; a program needn't handle non-finite values.
Results may differ from a plain program's by a relative error of at most 0.0012.
Values sent between devices are 32-bit elements; how exact they have to be, the bound alone decides.
No kernel may reach another device: no remote copies, remote signals or barrier semaphores. Data moves between devices by JAX's collectives and lax.ppermute only.
A program may use at most 64 MiB of HBM per device.

v0:
```python
import jax
import jax.numpy as jnp
from jax import lax
from jax.sharding import PartitionSpec as P

ITERS = 4


def extended(cells, sides, width):
    for axis, dim in sides:
        count = lax.axis_size(axis)
        ends = count - 1
        head = lax.slice_in_dim(cells, 0, width, axis=dim)
        tail = lax.slice_in_dim(cells, cells.shape[dim] - width, cells.shape[dim], axis=dim)
        cells = jnp.concatenate(
            [
                lax.ppermute(tail, axis, [(i, (i + 1) % count) for i in range(ends)]),
                cells,
                lax.ppermute(head, axis, [((i + 1) % count, i) for i in range(ends)]),
            ],
            axis=dim,
        )
    return cells


def expand(field):
    return extended(field, (("gx", 0), ("gy", 1)), 1)


def operate(field, matrix_tiles, tile_codes, tile_counts):
    padded = expand(field)
    height, breadth = (tile_codes.shape[0], tile_codes.shape[1])
    stacked = jnp.stack(
        [
            padded[1 + row_step : 1 + row_step + height, 1 + col_step : 1 + col_step + breadth]
            for row_step in (-1, 0, 1)
            for col_step in (-1, 0, 1)
        ]
    )
    present = (
        jnp.arange(tile_codes.shape[2], dtype=jnp.int32)[None, None, :] < tile_counts[:, :, None]
    )
    onehot = (tile_codes[:, :, :, None] == jnp.arange(9, dtype=jnp.int32)) & present[:, :, :, None]
    onehot = onehot.astype(jnp.float32)
    picked = jnp.einsum("xysc,cxyk->xysk", onehot, stacked, precision=lax.Precision.HIGHEST)
    return jnp.einsum("xyskl,xysl->xyk", matrix_tiles, picked, precision=lax.Precision.HIGHEST)


def solve_small(lower, target, steps):
    forward = []
    for row in range(steps):
        total = target[row]
        for column in range(row):
            total = total - lower[row, column] * forward[column]
        forward.append(total / lower[row, row])
    backward = [None] * steps
    for row in reversed(range(steps)):
        total = forward[row]
        for column in range(row + 1, steps):
            total = total - lower[column, row] * backward[column]
        backward[row] = total / lower[row, row]
    return backward


def body(matrix_tiles, tile_codes, tile_counts, right_side, initial_guess):
    start = right_side - operate(initial_guess, matrix_tiles, tile_codes, tile_counts)
    beta = jnp.sqrt(lax.psum(jnp.sum(start * start), ("gx", "gy")))
    basis = [start / beta]
    images = []
    hessenberg = jnp.zeros((ITERS + 1, ITERS), jnp.float32)
    for column in range(ITERS):
        vector_new = operate(basis[column], matrix_tiles, tile_codes, tile_counts)
        images.append(vector_new)
        stacked_basis = jnp.stack(basis)
        local_inner = jnp.einsum(
            "jxyk,xyk->j", stacked_basis, vector_new, precision=lax.Precision.HIGHEST
        )
        inners, whole_square = lax.psum(
            (local_inner, jnp.sum(vector_new * vector_new)), ("gx", "gy")
        )
        vector_new = vector_new - jnp.einsum(
            "j,jxyk->xyk", inners, stacked_basis, precision=lax.Precision.HIGHEST
        )
        hessenberg = hessenberg.at[: column + 1, column].set(inners)
        length_new = jnp.sqrt(whole_square - jnp.sum(inners * inners))
        hessenberg = hessenberg.at[column + 1, column].set(length_new)
        if column + 1 < ITERS:
            basis.append(vector_new / length_new)
    normal_matrix = jnp.dot(hessenberg.T, hessenberg, precision=lax.Precision.HIGHEST)
    target = beta * hessenberg[0, :]
    lower = jnp.linalg.cholesky(normal_matrix)
    weights = solve_small(lower, target, ITERS)
    solution = initial_guess
    for column in range(ITERS):
        solution = solution + weights[column] * basis[column]
    residual = right_side - operate(solution, matrix_tiles, tile_codes, tile_counts)
    return (solution, residual, hessenberg)


def solution(mesh):
    placed = (
        P("gx", "gy", None, None, None),
        P("gx", "gy", None),
        P("gx", "gy"),
        P("gx", "gy", None),
        P("gx", "gy", None),
    )
    return jax.shard_map(
        body,
        mesh=mesh,
        in_specs=placed,
        out_specs=(P("gx", "gy", None), P("gx", "gy", None), P()),
        check_vma=False,
    )
```

profile of v0, /device:TPU:0, one launch (start us, length us, event | category | flops | bytes accessed | tf_op | source)
XLA Modules:
  0.0 367.7 jit_solution(6675934290111600294)
XLA Ops:
  1.5 5.0 %collective-permute-start = (f32[1,4,128]{2,1,0:T(4,128)S(1)}, f32[1,4,128]{2,1,0:T(4,128)S(1)}, u32[]{:S(2)}, u32[]{:S(2)}) collective-permute-start(f32[1,4,128]{2,1,0:T(4,128)S(1)} %get-tuple-element.132), channel_id=1, source_target_pairs={{0,8},{8,16},{16,24},{1,9},{9,17},{17,25},{2,10},{10,18},{18,26},{... | collective-permute-start | bytes 6152 | tf_op jit(solution)/shard_map/ppermute | solution.py:17
  16.7 2.7 collective-permute-done.3
  21.7 2.7 fusion.23
  25.0 43.5 %psum.63 = f32[]{:T(128)} all-reduce(f32[]{:T(128)} %get-tuple-element.107), channel_id=1, replica_groups=mesh['gx'=4,'gy'=8] {'gx','gy'}, use_global_device_ids=true, to_apply=%region_1.0 | all-reduce | flops 1 | bytes 8 | tf_op jit(solution)/shard_map/psum | solution.py:67
  69.3 4.2 %collective-permute-start.4 = (f32[1,4,128]{2,1,0:T(4,128)S(1)}, f32[1,4,128]{2,1,0:T(4,128)S(1)}, u32[]{:S(2)}, u32[]{:S(2)}) collective-permute-start(f32[1,4,128]{2,1,0:T(4,128)S(1)} %get-tuple-element.129), channel_id=1, source_target_pairs={{0,8},{8,16},{16,24},{1,9},{9,17},{17,25},{2,10},{10,18},{18,26},{... | collective-permute-start | bytes 6152 | tf_op jit(solution)/shard_map/ppermute | solution.py:17
  74.8 4.2 %collective-permute-done.5 = f32[1,4,128]{2,1,0:T(4,128)S(1)} collective-permute-done((f32[1,4,128]{2,1,0:T(4,128)S(1)}, f32[1,4,128]{2,1,0:T(4,128)S(1)}, u32[]{:S(2)}, u32[]{:S(2)}) %collective-permute-start.5) | collective-permute-done | bytes 2080 | tf_op jit(solution)/shard_map/ppermute | solution.py:19
  82.8 2.5 collective-permute-done.7
  85.7 2.7 fusion.21
  89.6 42.2 %all-reduce.4 = (f32[]{:T(128)}, f32[1]{0:T(128)}) all-reduce(f32[]{:T(128)} %multiply_reduce_fusion.4, f32[1]{0:T(128)} %bitcast.28), channel_id=1, replica_groups=mesh['gx'=4,'gy'=8] {'gx','gy'}, use_global_device_ids=true, to_apply=%region_4.0 | all-reduce | flops 2 | bytes 16 | tf_op jit(solution)/shard_map/psum | solution.py:78
  134.5 4.2 %collective-permute-start.8 = (f32[1,4,128]{2,1,0:T(4,128)S(1)}, f32[1,4,128]{2,1,0:T(4,128)S(1)}, u32[]{:S(2)}, u32[]{:S(2)}) collective-permute-start(f32[1,4,128]{2,1,0:T(4,128)S(1)} %get-tuple-element.127), channel_id=1, source_target_pairs={{0,8},{8,16},{16,24},{1,9},{9,17},{17,25},{2,10},{10,18},{18,26},{... | collective-permute-start | bytes 6152 | tf_op jit(solution)/shard_map/ppermute | solution.py:17
  140.0 4.2 %collective-permute-done.9 = f32[1,4,128]{2,1,0:T(4,128)S(1)} collective-permute-done((f32[1,4,128]{2,1,0:T(4,128)S(1)}, f32[1,4,128]{2,1,0:T(4,128)S(1)}, u32[]{:S(2)}, u32[]{:S(2)}) %collective-permute-start.9) | collective-permute-done | bytes 2080 | tf_op jit(solution)/shard_map/ppermute | solution.py:19
  150.3 2.7 fusion.19
  153.9 42.3 %all-reduce.3 = (f32[2]{0:T(128)S(1)}, f32[]{:T(128)}) all-reduce(f32[2]{0:T(128)S(1)} %convolution_bitcast_fusion.8, f32[]{:T(128)} %multiply_reduce_fusion.3), channel_id=1, replica_groups=mesh['gx'=4,'gy'=8] {'gx','gy'}, use_global_device_ids=true, to_apply=%region_6.0 | all-reduce | flops 3 | bytes 24 | tf_op jit(solution)/shard_map/psum | solution.py:78
  198.3 4.2 %collective-permute-start.12 = (f32[1,4,128]{2,1,0:T(4,128)S(1)}, f32[1,4,128]{2,1,0:T(4,128)S(1)}, u32[]{:S(2)}, u32[]{:S(2)}) collective-permute-start(f32[1,4,128]{2,1,0:T(4,128)S(1)} %get-tuple-element.125), channel_id=1, source_target_pairs={{0,8},{8,16},{16,24},{1,9},{9,17},{17,25},{2,10},{10,18},{18,26},{... | collective-permute-start | bytes 6152 | tf_op jit(solution)/shard_map/ppermute | solution.py:17
  214.8 2.7 fusion.17
  218.4 42.3 %all-reduce.2 = (f32[3]{0:T(128)S(1)}, f32[]{:T(128)}) all-reduce(f32[3]{0:T(128)S(1)} %convolution_bitcast_fusion.7, f32[]{:T(128)} %multiply_reduce_fusion.2), channel_id=1, replica_groups=mesh['gx'=4,'gy'=8] {'gx','gy'}, use_global_device_ids=true, to_apply=%region_11.0 | all-reduce | flops 4 | bytes 32 | tf_op jit(solution)/shard_map/psum | solution.py:78
  262.8 4.2 %collective-permute-start.16 = (f32[1,4,128]{2,1,0:T(4,128)S(1)}, f32[1,4,128]{2,1,0:T(4,128)S(1)}, u32[]{:S(2)}, u32[]{:S(2)}) collective-permute-start(f32[1,4,128]{2,1,0:T(4,128)S(1)} %get-tuple-element.123), channel_id=1, source_target_pairs={{0,8},{8,16},{16,24},{1,9},{9,17},{17,25},{2,10},{10,18},{18,26},{... | collective-permute-start | bytes 6152 | tf_op jit(solution)/shard_map/ppermute | solution.py:17
  276.5 2.5 collective-permute-done.19
  279.4 2.7 fusion.15
  283.0 42.3 %all-reduce.1 = (f32[4]{0:T(128)S(1)}, f32[]{:T(128)}) all-reduce(f32[4]{0:T(128)S(1)} %convolution_bitcast_fusion.6, f32[]{:T(128)} %multiply_reduce_fusion.1), channel_id=1, replica_groups=mesh['gx'=4,'gy'=8] {'gx','gy'}, use_global_device_ids=true, to_apply=%region_16.0 | all-reduce | flops 5 | bytes 40 | tf_op jit(solution)/shard_map/psum | solution.py:78
  349.2 4.2 %collective-permute-start.20 = (f32[1,4,128]{2,1,0:T(4,128)S(1)}, f32[1,4,128]{2,1,0:T(4,128)S(1)}, u32[]{:S(2)}, u32[]{:S(2)}) collective-permute-start(f32[1,4,128]{2,1,0:T(4,128)S(1)} %get-tuple-element.121), channel_id=1, source_target_pairs={{0,8},{8,16},{16,24},{1,9},{9,17},{17,25},{2,10},{10,18},{18,26},{... | collective-permute-start | bytes 6152 | tf_op jit(solution)/shard_map/ppermute | solution.py:17
  354.7 4.2 %collective-permute-done.21 = f32[1,4,128]{2,1,0:T(4,128)S(1)} collective-permute-done((f32[1,4,128]{2,1,0:T(4,128)S(1)}, f32[1,4,128]{2,1,0:T(4,128)S(1)}, u32[]{:S(2)}, u32[]{:S(2)}) %collective-permute-start.21) | collective-permute-done | bytes 2080 | tf_op jit(solution)/shard_map/ppermute | solution.py:19
  361.5 2.5 collective-permute-done.23
  364.4 2.7 fusion.13
  (177 shorter events, 67.1 us)
Async XLA Ops:
  1.5 10.4 %collective-permute-start = (f32[1,4,128]{2,1,0:T(4,128)S(1)}, f32[1,4,128]{2,1,0:T(4,128)S(1)}, u32[]{:S(2)}, u32[]{:S(2)}) collective-permute-start(f32[1,4,128]{2,1,0:T(4,128)S(1)} %get-tuple-element.132), channel_id=1, source_target_pairs={{0,8},{8,16},{16,24},{1,9},{9,17},{17,25},{2,10},{10,18},{18,26},{... | collective-permute-start | bytes 6152 | tf_op jit(solution)/shard_map/ppermute | solution.py:17
  6.5 6.1 %collective-permute-start.1 = (f32[1,4,128]{2,1,0:T(4,128)S(1)}, f32[1,4,128]{2,1,0:T(4,128)S(1)}, u32[]{:S(2)}, u32[]{:S(2)}) collective-permute-start(f32[1,4,128]{2,1,0:T(4,128)S(1)} %get-tuple-element.131), channel_id=1, source_target_pairs={{8,0},{16,8},{24,16},{9,1},{17,9},{25,17},{10,2},{18,10},{26,18},{... | collective-permute-start | bytes 6152 | tf_op jit(solution)/shard_map/ppermute | solution.py:19
  12.6 3.3 collective-permute-start.2
  14.7 4.7 %collective-permute-start.3 = (f32[4,1,128]{2,1,0:T(1,128)S(1)}, f32[4,1,128]{2,1,0:T(1,128)S(1)}, u32[]{:S(2)}, u32[]{:S(2)}) collective-permute-start(f32[4,1,128]{2,1,0:T(1,128)S(1)} %get-tuple-element.119), channel_id=1, source_target_pairs={{1,0},{2,1},{3,2},{4,3},{5,4},{6,5},{7,6},{9,8},{10,9},{11,10},{12... | collective-permute-start | bytes 6152 | tf_op jit(solution)/shard_map/ppermute | solution.py:19
  69.3 5.5 %collective-permute-start.4 = (f32[1,4,128]{2,1,0:T(4,128)S(1)}, f32[1,4,128]{2,1,0:T(4,128)S(1)}, u32[]{:S(2)}, u32[]{:S(2)}) collective-permute-start(f32[1,4,128]{2,1,0:T(4,128)S(1)} %get-tuple-element.129), channel_id=1, source_target_pairs={{0,8},{8,16},{16,24},{1,9},{9,17},{17,25},{2,10},{10,18},{18,26},{... | collective-permute-start | bytes 6152 | tf_op jit(solution)/shard_map/ppermute | solution.py:17
  73.4 5.5 %collective-permute-start.5 = (f32[1,4,128]{2,1,0:T(4,128)S(1)}, f32[1,4,128]{2,1,0:T(4,128)S(1)}, u32[]{:S(2)}, u32[]{:S(2)}) collective-permute-start(f32[1,4,128]{2,1,0:T(4,128)S(1)} %get-tuple-element.130), channel_id=1, source_target_pairs={{8,0},{16,8},{24,16},{9,1},{17,9},{25,17},{10,2},{18,10},{26,18},{... | collective-permute-start | bytes 6152 | tf_op jit(solution)/shard_map/ppermute | solution.py:19
  78.9 3.8 %collective-permute-start.6 = (f32[4,1,128]{2,1,0:T(1,128)S(1)}, f32[4,1,128]{2,1,0:T(1,128)S(1)}, u32[]{:S(2)}, u32[]{:S(2)}) collective-permute-start(f32[4,1,128]{2,1,0:T(1,128)S(1)} %get-tuple-element.118), channel_id=1, source_target_pairs={{0,1},{1,2},{2,3},{3,4},{4,5},{5,6},{6,7},{8,9},{9,10},{10,11},{11... | collective-permute-start | bytes 6152 | tf_op jit(solution)/shard_map/ppermute | solution.py:17
  81.5 3.8 %collective-permute-start.7 = (f32[4,1,128]{2,1,0:T(1,128)S(1)}, f32[4,1,128]{2,1,0:T(1,128)S(1)}, u32[]{:S(2)}, u32[]{:S(2)}) collective-permute-start(f32[4,1,128]{2,1,0:T(1,128)S(1)} %get-tuple-element.117), channel_id=1, source_target_pairs={{1,0},{2,1},{3,2},{4,3},{5,4},{6,5},{7,6},{9,8},{10,9},{11,10},{12... | collective-permute-start | bytes 6152 | tf_op jit(solution)/shard_map/ppermute | solution.py:19
  134.5 5.5 %collective-permute-start.8 = (f32[1,4,128]{2,1,0:T(4,128)S(1)}, f32[1,4,128]{2,1,0:T(4,128)S(1)}, u32[]{:S(2)}, u32[]{:S(2)}) collective-permute-start(f32[1,4,128]{2,1,0:T(4,128)S(1)} %get-tuple-element.127), channel_id=1, source_target_pairs={{0,8},{8,16},{16,24},{1,9},{9,17},{17,25},{2,10},{10,18},{18,26},{... | collective-permute-start | bytes 6152 | tf_op jit(solution)/shard_map/ppermute | solution.py:17
  138.7 5.5 %collective-permute-start.9 = (f32[1,4,128]{2,1,0:T(4,128)S(1)}, f32[1,4,128]{2,1,0:T(4,128)S(1)}, u32[]{:S(2)}, u32[]{:S(2)}) collective-permute-start(f32[1,4,128]{2,1,0:T(4,128)S(1)} %get-tuple-element.128), channel_id=1, source_target_pairs={{8,0},{16,8},{24,16},{9,1},{17,9},{25,17},{10,2},{18,10},{26,18},{... | collective-permute-start | bytes 6152 | tf_op jit(solution)/shard_map/ppermute | solution.py:19
  144.1 3.3 collective-permute-start.10
  146.1 3.8 %collective-permute-start.11 = (f32[4,1,128]{2,1,0:T(1,128)S(1)}, f32[4,1,128]{2,1,0:T(1,128)S(1)}, u32[]{:S(2)}, u32[]{:S(2)}) collective-permute-start(f32[4,1,128]{2,1,0:T(1,128)S(1)} %get-tuple-element.115), channel_id=1, source_target_pairs={{1,0},{2,1},{3,2},{4,3},{5,4},{6,5},{7,6},{9,8},{10,9},{11,10},{12... | collective-permute-start | bytes 6152 | tf_op jit(solution)/shard_map/ppermute | solution.py:19
  198.3 7.3 %collective-permute-start.12 = (f32[1,4,128]{2,1,0:T(4,128)S(1)}, f32[1,4,128]{2,1,0:T(4,128)S(1)}, u32[]{:S(2)}, u32[]{:S(2)}) collective-permute-start(f32[1,4,128]{2,1,0:T(4,128)S(1)} %get-tuple-element.125), channel_id=1, source_target_pairs={{0,8},{8,16},{16,24},{1,9},{9,17},{17,25},{2,10},{10,18},{18,26},{... | collective-permute-start | bytes 6152 | tf_op jit(solution)/shard_map/ppermute | solution.py:17
  202.5 5.5 %collective-permute-start.13 = (f32[1,4,128]{2,1,0:T(4,128)S(1)}, f32[1,4,128]{2,1,0:T(4,128)S(1)}, u32[]{:S(2)}, u32[]{:S(2)}) collective-permute-start(f32[1,4,128]{2,1,0:T(4,128)S(1)} %get-tuple-element.126), channel_id=1, source_target_pairs={{8,0},{16,8},{24,16},{9,1},{17,9},{25,17},{10,2},{18,10},{26,18},{... | collective-permute-start | bytes 6152 | tf_op jit(solution)/shard_map/ppermute | solution.py:19
  208.0 4.1 %collective-permute-start.14 = (f32[4,1,128]{2,1,0:T(1,128)S(1)}, f32[4,1,128]{2,1,0:T(1,128)S(1)}, u32[]{:S(2)}, u32[]{:S(2)}) collective-permute-start(f32[4,1,128]{2,1,0:T(1,128)S(1)} %get-tuple-element.114), channel_id=1, source_target_pairs={{0,1},{1,2},{2,3},{3,4},{4,5},{5,6},{6,7},{8,9},{9,10},{10,11},{11... | collective-permute-start | bytes 6152 | tf_op jit(solution)/shard_map/ppermute | solution.py:17
  210.6 3.9 %collective-permute-start.15 = (f32[4,1,128]{2,1,0:T(1,128)S(1)}, f32[4,1,128]{2,1,0:T(1,128)S(1)}, u32[]{:S(2)}, u32[]{:S(2)}) collective-permute-start(f32[4,1,128]{2,1,0:T(1,128)S(1)} %get-tuple-element.113), channel_id=1, source_target_pairs={{1,0},{2,1},{3,2},{4,3},{5,4},{6,5},{7,6},{9,8},{10,9},{11,10},{12... | collective-permute-start | bytes 6152 | tf_op jit(solution)/shard_map/ppermute | solution.py:19
  262.8 7.4 %collective-permute-start.16 = (f32[1,4,128]{2,1,0:T(4,128)S(1)}, f32[1,4,128]{2,1,0:T(4,128)S(1)}, u32[]{:S(2)}, u32[]{:S(2)}) collective-permute-start(f32[1,4,128]{2,1,0:T(4,128)S(1)} %get-tuple-element.123), channel_id=1, source_target_pairs={{0,8},{8,16},{16,24},{1,9},{9,17},{17,25},{2,10},{10,18},{18,26},{... | collective-permute-start | bytes 6152 | tf_op jit(solution)/shard_map/ppermute | solution.py:17
  267.0 5.5 %collective-permute-start.17 = (f32[1,4,128]{2,1,0:T(4,128)S(1)}, f32[1,4,128]{2,1,0:T(4,128)S(1)}, u32[]{:S(2)}, u32[]{:S(2)}) collective-permute-start(f32[1,4,128]{2,1,0:T(4,128)S(1)} %get-tuple-element.124), channel_id=1, source_target_pairs={{8,0},{16,8},{24,16},{9,1},{17,9},{25,17},{10,2},{18,10},{26,18},{... | collective-permute-start | bytes 6152 | tf_op jit(solution)/shard_map/ppermute | solution.py:19
  272.5 4.0 %collective-permute-start.18 = (f32[4,1,128]{2,1,0:T(1,128)S(1)}, f32[4,1,128]{2,1,0:T(1,128)S(1)}, u32[]{:S(2)}, u32[]{:S(2)}) collective-permute-start(f32[4,1,128]{2,1,0:T(1,128)S(1)} %get-tuple-element.112), channel_id=1, source_target_pairs={{0,1},{1,2},{2,3},{3,4},{4,5},{5,6},{6,7},{8,9},{9,10},{10,11},{11... | collective-permute-start | bytes 6152 | tf_op jit(solution)/shard_map/ppermute | solution.py:17
  275.2 3.9 %collective-permute-start.19 = (f32[4,1,128]{2,1,0:T(1,128)S(1)}, f32[4,1,128]{2,1,0:T(1,128)S(1)}, u32[]{:S(2)}, u32[]{:S(2)}) collective-permute-start(f32[4,1,128]{2,1,0:T(1,128)S(1)} %get-tuple-element.111), channel_id=1, source_target_pairs={{1,0},{2,1},{3,2},{4,3},{5,4},{6,5},{7,6},{9,8},{10,9},{11,10},{12... | collective-permute-start | bytes 6152 | tf_op jit(solution)/shard_map/ppermute | solution.py:19
  349.2 5.5 %collective-permute-start.20 = (f32[1,4,128]{2,1,0:T(4,128)S(1)}, f32[1,4,128]{2,1,0:T(4,128)S(1)}, u32[]{:S(2)}, u32[]{:S(2)}) collective-permute-start(f32[1,4,128]{2,1,0:T(4,128)S(1)} %get-tuple-element.121), channel_id=1, source_target_pairs={{0,8},{8,16},{16,24},{1,9},{9,17},{17,25},{2,10},{10,18},{18,26},{... | collective-permute-start | bytes 6152 | tf_op jit(solution)/shard_map/ppermute | solution.py:17
  353.4 5.5 %collective-permute-start.21 = (f32[1,4,128]{2,1,0:T(4,128)S(1)}, f32[1,4,128]{2,1,0:T(4,128)S(1)}, u32[]{:S(2)}, u32[]{:S(2)}) collective-permute-start(f32[1,4,128]{2,1,0:T(4,128)S(1)} %get-tuple-element.122), channel_id=1, source_target_pairs={{8,0},{16,8},{24,16},{9,1},{17,9},{25,17},{10,2},{18,10},{26,18},{... | collective-permute-start | bytes 6152 | tf_op jit(solution)/shard_map/ppermute | solution.py:19
  358.9 2.6 collective-permute-start.22
  360.2 3.9 %collective-permute-start.23 = (f32[4,1,128]{2,1,0:T(1,128)S(1)}, f32[4,1,128]{2,1,0:T(1,128)S(1)}, u32[]{:S(2)}, u32[]{:S(2)}) collective-permute-start(f32[4,1,128]{2,1,0:T(1,128)S(1)} %get-tuple-element.109), channel_id=1, source_target_pairs={{1,0},{2,1},{3,2},{4,3},{5,4},{6,5},{7,6},{9,8},{10,9},{11,10},{12... | collective-permute-start | bytes 6152 | tf_op jit(solution)/shard_map/ppermute | solution.py:19
  (6 other events, 319.5 us)
where the time goes:
time: 372 us; the launch traced here: 368 us
  blocking collectives  213 us (57%)
  starting transfers between devices  49.4 us (13%)
  waiting for transfers between devices  32.2 us (9%)
  between operations  23.4 us (6%)
  other arithmetic  20.5 us (6%)
  matrix products  19 us (5%)
  local copies, waits for them, and re-layouts  10.7 us (3%)
    psum x4, blocking collectives, body(): lax.psum((local_inner, jnp.sum(vector_new * vector_new)), ('gx', 'gy'))  169 us
    psum x1, blocking collectives, body(): beta = jnp.sqrt(lax.psum(jnp.sum(start * start), ('gx', 'gy')))  43.5 us
    ppermute x12, starting transfers between devices, extended(): lax.ppermute(tail, axis, [(i, (i + 1) % count) for i in range(ends)])  33.8 us
    ppermute x12, waiting for transfers between devices, extended(): lax.ppermute(head, axis, [((i + 1) % count, i) for i in range(ends)])  32.1 us
    dot_general x6, matrix products, operate(): jnp.einsum('xyskl,xysl->xyk', matrix_tiles, picked, precision=lax.Precisi...  16 us
    ppermute x12, starting transfers between devices, extended(): lax.ppermute(head, axis, [((i + 1) % count, i) for i in range(ends)])  15.7 us
    another operation x8, other arithmetic  9.14 us
  transfers between devices with their start and end apart: 24, of which 11 were waited for; matrix products, arithmetic and copies ran while one was open for 4% of the time, Pallas kernels for 0%

commit v1 on v0

v1 whole, which is shorter than its diff:
```python
import functools

import jax
import jax.numpy as jnp
from jax import lax
from jax.experimental import pallas as pl
from jax.experimental.pallas import tpu as pltpu
from jax.sharding import PartitionSpec as P

ITERS = 4
AXES = ("gx", "gy")
VMEM_BYTES = 12 * 1024 * 1024
OFFSETS = [(dx, dy) for dx in (-1, 0, 1) for dy in (-1, 0, 1) if (dx, dy) != (0, 0)]


class Shape:
    def __init__(self, codes):
        self.rx, self.ry, self.slots = codes.shape
        self.nb = self.rx * self.ry
        self.nx = lax.axis_size("gx")
        self.ny = lax.axis_size("gy")
        self.nd = self.nx * self.ny
        self.rows = max(self.rx, self.ry) + 1
        self.width = self.ry + 2
        self.zero = (self.rx + 2) * (self.ry + 2)

    def edge(self, dx, dy):
        xs = {-1: [0], 0: range(self.rx), 1: [self.rx - 1]}[dx]
        ys = {-1: [0], 0: range(self.ry), 1: [self.ry - 1]}[dy]
        return [(x, y) for x in xs for y in ys]

    def halo(self, dx, dy):
        xs = {-1: [0], 0: range(1, self.rx + 1), 1: [self.rx + 1]}[dx]
        ys = {-1: [0], 0: range(1, self.ry + 1), 1: [self.ry + 1]}[dy]
        return [x * self.width + y for x in xs for y in ys]


def neighbour(shape, ix, iy, dx, dy):
    x, y = ix + dx, iy + dy
    inside = (x >= 0) & (x < shape.nx) & (y >= 0) & (y < shape.ny)
    return jnp.where(inside, x * shape.ny + y, ix * shape.ny + iy)


def pack(shape, here, rows, send):
    for dx, dy in OFFSETS:
        dst = neighbour(shape, here[0], here[1], dx, dy)
        for k, (x, y) in enumerate(shape.edge(dx, dy)):
            send[dst, k] = rows[x * shape.ry + y]


def unpack(shape, here, recv, own, padded):
    for x in range(shape.rx):
        for y in range(shape.ry):
            padded[(x + 1) * shape.width + y + 1] = own[x * shape.ry + y]
    for dx, dy in OFFSETS:
        src = neighbour(shape, here[0], here[1], dx, dy)
        for k, position in enumerate(shape.halo(dx, dy)):
            padded[position] = recv[src, k]
    padded[shape.zero] = jnp.zeros_like(padded[shape.zero])


def matvec(shape, index, tiles, padded):
    blk = tiles.shape[-1]
    eye = lax.broadcasted_iota(jnp.int32, (blk, blk), 0) == lax.broadcasted_iota(
        jnp.int32, (blk, blk), 1
    )
    out = []
    for b in range(shape.nb):
        x, y = divmod(b, shape.ry)
        total = None
        for s in range(shape.slots):
            term = tiles[x, y, s] * padded[index[b, s]]
            total = term if total is None else total + term
        column = jnp.sum(total, axis=1, keepdims=True)
        out.append(jnp.sum(jnp.where(eye, column, 0.0), axis=0, keepdims=True))
    return jnp.concatenate(out, axis=0)


def inner(a, b):
    return jnp.sum(jnp.sum(a * b, axis=1, keepdims=True), axis=0, keepdims=True)


def spread(values):
    lane = lax.broadcasted_iota(jnp.int32, (1, 128), 1)
    row = jnp.zeros((1, 128), jnp.float32)
    for i, value in enumerate(values):
        row = jnp.where(lane == i, value, row)
    return row


def send_dots(shape, row, send):
    for d in range(shape.nd):
        send[d, shape.rows - 1] = row


def sum_dots(shape, recv, at, count):
    parts = [recv[d, at] for d in range(shape.nd)]
    while len(parts) > 1:
        parts = [a + b for a, b in zip(parts[::2], parts[1::2])] + (
            [parts[-1]] if len(parts) % 2 else []
        )
    return [parts[0][:, i : i + 1] for i in range(count)]


def split(value):
    return [value[b : b + 1] for b in range(value.shape[0])]


def first_kernel(shape, here, guess, send):
    rows = [guess[b : b + 1, :] for b in range(shape.nb)]
    pack(shape, here, rows, send)


def start_kernel(shape, here, index, tiles, recv, guess, right, send, start, padded):
    unpack(shape, here, recv, [guess[b : b + 1, :] for b in range(shape.nb)], padded)
    r = right[...] - matvec(shape, index, tiles, padded)
    start[...] = r
    pack(shape, here, split(r), send)
    send_dots(shape, spread([inner(r, r)]), send)


def step_kernel(shape, step, here, index, tiles, recv, *refs):
    keep, (send, v_out, w_out, *h_out, padded) = refs[: 2 * step + 1], refs[2 * step + 1 :]
    last = keep[-1]
    unpack(shape, here, recv, split(last[...]), padded)
    image = matvec(shape, index, tiles, padded)
    sums = sum_dots(shape, recv, shape.rows - 1, step + 1)
    square = sums[step]
    if step == 0:
        length = jnp.sqrt(square)
        scale = 1.0 / length
        v = last[...] * scale
        w = image * scale
        basis = []
    else:
        for i in range(step):
            square = square - sums[i] * sums[i]
        length = jnp.sqrt(square)
        scale = 1.0 / length
        basis = [ref[...] for ref in keep[1 : step + 1]]
        images = [ref[...] for ref in keep[step + 1 :]]
        v = images[-1]
        w = image
        for i in range(step):
            v = v - sums[i] * basis[i]
            w = w - sums[i] * images[i]
        v = v * scale
        w = w * scale
    v_out[...] = v
    w_out[...] = w
    h_out[0][...] = spread(sums[:step] + [length])
    if step + 1 < ITERS:
        pack(shape, here, split(w), send)
    dots = [inner(w, other) for other in basis + [v, w]]
    row = spread(dots)
    if step + 1 < ITERS:
        send_dots(shape, row, send)
    else:
        for d in range(shape.nd):
            send[d, 0] = row


def last_kernel(shape, recv, guess, start, *refs):
    vs, ws, hs, (solution, residual, hess) = (
        refs[:ITERS],
        refs[ITERS : 2 * ITERS],
        refs[2 * ITERS : 3 * ITERS],
        refs[3 * ITERS :],
    )
    sums = sum_dots(shape, recv, 0, ITERS + 1)
    square = sums[ITERS]
    for i in range(ITERS):
        square = square - sums[i] * sums[i]
    columns = []
    beta = hs[0][:, 0:1]
    for j in range(1, ITERS):
        columns.append([hs[j][:, i : i + 1] for i in range(j + 1)])
    columns.append(sums[:ITERS] + [jnp.sqrt(square)])
    hess[...] = jnp.zeros_like(hess)
    row = lax.broadcasted_iota(jnp.int32, hess.shape, 0)
    col = lax.broadcasted_iota(jnp.int32, hess.shape, 1)
    full = jnp.zeros(hess.shape, jnp.float32)
    for j, column in enumerate(columns):
        for i, value in enumerate(column):
            full = jnp.where((row == i) & (col == j), value, full)
    hess[...] = full
    normal = {}
    for a in range(ITERS):
        for b in range(a + 1):
            total = None
            for p, q in zip(columns[a], columns[b]):
                total = p * q if total is None else total + p * q
            normal[a, b] = total
    lower, inverse = {}, {}
    for a in range(ITERS):
        for b in range(a + 1):
            total = normal[a, b]
            for c in range(b):
                total = total - lower[a, c] * lower[b, c]
            if a == b:
                inverse[a] = lax.rsqrt(total)
            else:
                lower[a, b] = total * inverse[b]
    forward = []
    for a in range(ITERS):
        total = beta * columns[a][0]
        for c in range(a):
            total = total - lower[a, c] * forward[c]
        forward.append(total * inverse[a])
    weights = [None] * ITERS
    for a in reversed(range(ITERS)):
        total = forward[a]
        for c in range(a + 1, ITERS):
            total = total - lower[c, a] * weights[c]
        weights[a] = total * inverse[a]
    x = guess[...]
    r = start[...]
    for j in range(ITERS):
        x = x + weights[j] * vs[j][...]
        r = r - weights[j] * ws[j][...]
    solution[...] = x
    residual[...] = r


def table(shape, here, codes, counts):
    x = jnp.arange(shape.rx, dtype=jnp.int32)[:, None, None] + codes // 3
    y = jnp.arange(shape.ry, dtype=jnp.int32)[None, :, None] + codes % 3
    gx = here[0] * shape.rx + x - 1
    gy = here[1] * shape.ry + y - 1
    live = jnp.arange(shape.slots, dtype=jnp.int32) < counts[:, :, None]
    live &= (gx >= 0) & (gx < shape.nx * shape.rx) & (gy >= 0) & (gy < shape.ny * shape.ry)
    return jnp.where(live, x * shape.width + y, shape.zero).reshape(shape.nb, shape.slots)


def body(tiles, codes, counts, right_side, initial_guess):
    shape = Shape(codes)
    blk = tiles.shape[-1]
    here = jnp.stack([lax.axis_index("gx"), lax.axis_index("gy")]).astype(jnp.int32)
    index = table(shape, here, codes, counts)
    flat = (shape.nb, blk)
    guess = initial_guess.reshape(flat)
    right = right_side.reshape(flat)
    smem = pl.BlockSpec(memory_space=pltpu.SMEM)
    vmem = pl.BlockSpec(memory_space=pltpu.VMEM)
    vector = jax.ShapeDtypeStruct(flat, jnp.float32)
    small = jax.ShapeDtypeStruct((1, blk), jnp.float32)
    buffer = jax.ShapeDtypeStruct((shape.nd, shape.rows, 1, blk), jnp.float32)
    params = pltpu.CompilerParams(vmem_limit_bytes=VMEM_BYTES)
    padded = pltpu.VMEM((shape.zero + 1, 1, blk), jnp.float32)

    def exchange(send):
        return lax.all_to_all(send, AXES, 0, 0, tiled=True)

    send = pl.pallas_call(
        functools.partial(first_kernel, shape),
        out_shape=buffer,
        in_specs=[smem, vmem],
        out_specs=vmem,
        compiler_params=params,
        name="first",
    )(here, guess)
    recv = exchange(send)
    send, start = pl.pallas_call(
        functools.partial(start_kernel, shape),
        out_shape=(buffer, vector),
        in_specs=[smem, smem, vmem, vmem, vmem, vmem],
        out_specs=(vmem, vmem),
        scratch_shapes=[padded],
        compiler_params=params,
        name="start",
    )(here, index, tiles, recv, guess, right)
    vs, ws, hs = [], [], []
    for step in range(ITERS):
        recv = exchange(send)
        keep = [start, *vs, *ws]
        final = step + 1 == ITERS
        out = buffer if not final else jax.ShapeDtypeStruct((shape.nd, 1, 1, blk), jnp.float32)
        send, v, w, h = pl.pallas_call(
            functools.partial(step_kernel, shape, step),
            out_shape=(out, vector, vector, small),
            in_specs=[smem, smem] + [vmem] * (2 + len(keep)),
            out_specs=(vmem,) * 4,
            scratch_shapes=[padded],
            compiler_params=params,
            name=f"step{step}",
        )(here, index, tiles, recv, *keep)
        vs.append(v)
        ws.append(w)
        hs.append(h)
    recv = exchange(send)
    solution, residual, hessenberg = pl.pallas_call(
        functools.partial(last_kernel, shape),
        out_shape=(vector, vector, jax.ShapeDtypeStruct((ITERS + 1, ITERS), jnp.float32)),
        in_specs=[vmem] * (3 + 3 * ITERS),
        out_specs=(vmem,) * 3,
        compiler_params=params,
        name="last",
    )(recv, guess, start, *vs, *ws, *hs)
    whole = initial_guess.shape
    return solution.reshape(whole), residual.reshape(whole), hessenberg


def solution(mesh):
    placed = (
        P("gx", "gy", None, None, None),
        P("gx", "gy", None),
        P("gx", "gy"),
        P("gx", "gy", None),
        P("gx", "gy", None),
    )
    return jax.shard_map(
        body,
        mesh=mesh,
        in_specs=placed,
        out_specs=(P("gx", "gy", None), P("gx", "gy", None), P()),
        check_vma=False,
    )
```

time: 372 us -> 74.1 us (0.20); the launches traced: 368 us -> 73.7 us
  blocking collectives: 213 us -> 45.9 us
  starting transfers between devices: 49.4 us -> 7.33 us
  waiting for transfers between devices: 32.2 us -> 6.77 us
  between operations: 23.4 us -> 0.7 us
  other arithmetic: 20.5 us -> 0.85 us
  matrix products: 19 us -> 0 us
  Pallas kernels: 0 us -> 7.55 us
  local copies, waits for them, and re-layouts: 10.7 us -> 4.62 us
    psum x5 -> x0, blocking collectives: 213 us -> none  [the longest x4 169 us: body(): lax.psum((local_inner, jnp.sum(vector_new * vector_new)), ('gx', 'gy'))]
    ppermute x24 -> x0, starting transfers between devices: 49.4 us -> none  [the longest x12 33.8 us: extended(): lax.ppermute(tail, axis, [(i, (i + 1) % count) for i in range(ends)])]
    all_to_all x0 -> x5, blocking collectives: none -> 45.9 us  [exchange(): return lax.all_to_all(send, AXES, 0, 0, tiled=True)]
    ppermute x24 -> x0, waiting for transfers between devices: 32.2 us -> none  [the longest x12 32.1 us: extended(): lax.ppermute(head, axis, [((i + 1) % count, i) for i in range(ends)])]
    dot_general x18 -> x0, matrix products: 19 us -> none  [the longest x6 16 us: operate(): jnp.einsum('xyskl,xysl->xyk', matrix_tiles, picked, precision=lax.Precisi...]
    another operation x21 -> x1, other arithmetic: 10.3 us -> 0.08 us  [body(): jnp.stack([lax.axis_index('gx'), lax.axis_index('gy')]).astype(jnp.int32)]
    pallas_call x0 -> x7, Pallas kernels: none -> 7.55 us  [the longest x4 4.41 us: body(): pl.pallas_call(functools.partial(step_kernel, shape, step), out_shape=(ou...]
    all_to_all x0 -> x1, starting transfers between devices: none -> 7.33 us  [exchange(): return lax.all_to_all(send, AXES, 0, 0, tiled=True)]
  transfers between devices with their start and end apart: 24 -> 1, of which waited for: 11 -> 1; matrix products, arithmetic and copies ran while one was open for 4% -> 1% of each run, Pallas kernels for 0% -> 0%
where the time goes in v1:
time: 74.1 us; the launch traced here: 73.7 us
  blocking collectives  45.9 us (62%)
  Pallas kernels  7.55 us (10%)
  starting transfers between devices  7.33 us (10%)
  waiting for transfers between devices  6.77 us (9%)
  local copies, waits for them, and re-layouts  4.62 us (6%)
  other arithmetic  0.85 us (1%)
    all_to_all x5, blocking collectives, exchange(): return lax.all_to_all(send, AXES, 0, 0, tiled=True)  45.9 us
    all_to_all x1, starting transfers between devices, exchange(): return lax.all_to_all(send, AXES, 0, 0, tiled=True)  7.33 us
    all_to_all x1, waiting for transfers between devices, exchange(): return lax.all_to_all(send, AXES, 0, 0, tiled=True)  6.77 us
    unnamed x13, local copies, waits for them, and re-layouts  4.62 us
    pallas_call x4, Pallas kernels, body(): pl.pallas_call(functools.partial(step_kernel, shape, step), out_shape=(ou...  4.41 us
  transfers between devices with their start and end apart: 1, of which 1 were waited for; matrix products, arithmetic and copies ran while one was open for 1% of the time, Pallas kernels for 0%

profile of v1, /device:TPU:0, one launch (start us, length us, event | category | flops | bytes accessed | tf_op | source)
XLA Modules:
  0.0 73.7 jit_solution(3298470268632631481)
XLA Ops:
  0.6 0.1 pad_add_fusion.here
  0.7 0.0 copy-start.2
  0.7 0.7 copy-done.2
  1.4 1.2 %first.1 = f32[32,5,1,128]{3,2,1,0:T(1,128)} custom-call(s32[2]{0:T(128)S(1)} %pad_add_fusion.here, f32[8,128]{1,0:T(8,128)S(1)} %bitcast.12), custom_call_target="tpu_custom_call" | custom-call | tf_op jit(solution)/shard_map/first/pallas_call | solution.py:254
  2.6 7.3 %all-to-all-start = ((f32[32,5,1,128]{3,2,1,0:T(1,128)}), f32[32,5,1,128]{3,2,1,0:T(1,128)S(1)}, u32[]{:S(2)}, u32[]{:S(2)}) async-start(f32[32,5,1,128]{3,2,1,0:T(1,128)} %first.1), calls=%async_computation | async-start | bytes 163840 | tf_op jit(solution)/shard_map/all_to_all | solution.py:252
  9.9 0.8 %add_select_fusion.2 = s32[2,4,6]{2,1,0:T(4,128)S(1)} fusion(s32[2,4,6]{2,1,0:T(4,128)} %param.6, s32[]{:T(128)S(6)} %mul.13, s32[]{:T(128)S(6)} %mul.12, s32[2,4]{1,0:T(2,128)} %param.7), kind=kLoop, calls=%fused_computation.4 | loop fusion | flops 1440 | bytes 424 | tf_op jit(solution)/shard_map/jit(_where)/select_n | solution.py:232
  10.7 6.8 %all-to-all-done.recv = f32[32,5,1,128]{3,2,1,0:T(1,128)S(1)} async-done(((f32[32,5,1,128]{3,2,1,0:T(1,128)}), f32[32,5,1,128]{3,2,1,0:T(1,128)S(1)}, u32[]{:S(2)}, u32[]{:S(2)}) %all-to-all-start) | async-done | bytes 81952 | tf_op jit(solution)/shard_map/all_to_all | solution.py:252
  17.5 1.9 %copy-done = f32[2,4,6,128,128]{4,3,2,1,0:T(8,128)S(1)} copy-done((f32[2,4,6,128,128]{4,3,2,1,0:T(8,128)S(1)}, f32[2,4,6,128,128]{4,3,2,1,0:T(8,128)}, u32[]{:S(2)}) %copy-start) | copy-done | bytes 3145752
  19.4 0.7 copy-done.3
  20.1 0.7 copy-done.5
  20.7 1.1 %start.1 = (f32[32,5,1,128]{3,2,1,0:T(1,128)S(1)}, f32[8,128]{1,0:T(8,128)S(1)}) custom-call(s32[2]{0:T(128)S(1)} %pad_add_fusion.here, s32[8,6]{1,0:T(8,128)S(1)} %bitcast.7, f32[2,4,6,128,128]{4,3,2,1,0:T(8,128)S(1)} %copy-done, f32[32,5,1,128]{3,2,1,0:T(1,128)S(1)} %all-to-all-done.recv, f32[8,128]{1,0:T(8,128)S(1)} %bitcast.13, f32[8,128]{1,0:T(8,128)S(1)} %bitcast.15), custom_call_target="tpu_custom_call" | custom-call | tf_op jit(solution)/shard_map/start/pallas_call | solution.py:263
  21.8 9.2 %all_to_all.30.recv = f32[32,5,1,128]{3,2,1,0:T(1,128)S(1)} all-to-all(f32[32,5,1,128]{3,2,1,0:T(1,128)S(1)} %get-tuple-element.24), channel_id=1, replica_groups=mesh['gx'=4,'gy'=8] {'gx','gy'}, dimensions={0} | all-to-all | bytes 163840 | tf_op jit(solution)/shard_map/all_to_all | solution.py:252
  31.1 0.0 copy-done.1
  31.1 1.1 %step0.1 = (f32[32,5,1,128]{3,2,1,0:T(1,128)S(1)}, f32[8,128]{1,0:T(8,128)S(1)}, f32[8,128]{1,0:T(8,128)S(1)}, f32[1,128]{1,0:T(1,128)S(1)}) custom-call(s32[2]{0:T(128)S(1)} %pad_add_fusion.here, s32[8,6]{1,0:T(8,128)S(1)} %bitcast.8, f32[2,4,6,128,128]{4,3,2,1,0:T(8,128)S(1)} %copy-done.1, f32[32,5,1,128]{3,2,1,0:T(1,128)S(1)} %all_to_all.30.recv, ...), custom_call_target="tpu_custom_call" | custom-call | tf_op jit(solution)/shard_map/step0/pallas_call | solution.py:278
  32.2 9.2 %all_to_all.31.recv = f32[32,5,1,128]{3,2,1,0:T(1,128)S(1)} all-to-all(f32[32,5,1,128]{3,2,1,0:T(1,128)S(1)} %get-tuple-element.26), channel_id=1, replica_groups=mesh['gx'=4,'gy'=8] {'gx','gy'}, dimensions={0} | all-to-all | bytes 163840 | tf_op jit(solution)/shard_map/all_to_all | solution.py:252
  41.4 1.1 %step1.1 = (f32[32,5,1,128]{3,2,1,0:T(1,128)S(1)}, f32[8,128]{1,0:T(8,128)S(1)}, f32[8,128]{1,0:T(8,128)S(1)}, f32[1,128]{1,0:T(1,128)S(1)}) custom-call(s32[2]{0:T(128)S(1)} %pad_add_fusion.here, s32[8,6]{1,0:T(8,128)S(1)} %bitcast.9, f32[2,4,6,128,128]{4,3,2,1,0:T(8,128)S(1)} %copy-done.1, f32[32,5,1,128]{3,2,1,0:T(1,128)S(1)} %all_to_all.31.recv, ...), custom_call_target="tpu_custom_call" | custom-call | tf_op jit(solution)/shard_map/step1/pallas_call | solution.py:278
  42.5 9.2 %all_to_all.32.recv = f32[32,5,1,128]{3,2,1,0:T(1,128)S(1)} all-to-all(f32[32,5,1,128]{3,2,1,0:T(1,128)S(1)} %get-tuple-element.29), channel_id=1, replica_groups=mesh['gx'=4,'gy'=8] {'gx','gy'}, dimensions={0} | all-to-all | bytes 163840 | tf_op jit(solution)/shard_map/all_to_all | solution.py:252
  51.8 1.1 %step2.1 = (f32[32,5,1,128]{3,2,1,0:T(1,128)S(1)}, f32[8,128]{1,0:T(8,128)S(1)}, f32[8,128]{1,0:T(8,128)S(1)}, f32[1,128]{1,0:T(1,128)S(1)}) custom-call(s32[2]{0:T(128)S(1)} %pad_add_fusion.here, s32[8,6]{1,0:T(8,128)S(1)} %bitcast.10, f32[2,4,6,128,128]{4,3,2,1,0:T(8,128)S(1)} %copy-done.1, f32[32,5,1,128]{3,2,1,0:T(1,128)S(1)} %all_to_all.32.recv, ...), custom_call_target="tpu_custom_call" | custom-call | tf_op jit(solution)/shard_map/step2/pallas_call | solution.py:278
  52.9 9.2 %all_to_all.33.recv = f32[32,5,1,128]{3,2,1,0:T(1,128)S(1)} all-to-all(f32[32,5,1,128]{3,2,1,0:T(1,128)S(1)} %get-tuple-element.32), channel_id=1, replica_groups=mesh['gx'=4,'gy'=8] {'gx','gy'}, dimensions={0} | all-to-all | bytes 163840 | tf_op jit(solution)/shard_map/all_to_all | solution.py:252
  62.2 1.1 %step3.1 = (f32[32,1,1,128]{3,2,1,0:T(1,128)S(1)}, f32[8,128]{1,0:T(8,128)S(1)}, f32[8,128]{1,0:T(8,128)S(1)}, f32[1,128]{1,0:T(1,128)S(1)}) custom-call(s32[2]{0:T(128)S(1)} %pad_add_fusion.here, s32[8,6]{1,0:T(8,128)S(1)} %bitcast.11, f32[2,4,6,128,128]{4,3,2,1,0:T(8,128)S(1)} %copy-done.1, f32[32,5,1,128]{3,2,1,0:T(1,128)S(1)} %all_to_all.33.recv, ...), custom_call_target="tpu_custom_call" | custom-call | tf_op jit(solution)/shard_map/step3/pallas_call | solution.py:278
  63.3 8.9 %all_to_all.34.recv = f32[32,1,1,128]{3,2,1,0:T(1,128)S(1)} all-to-all(f32[32,1,1,128]{3,2,1,0:T(1,128)S(1)} %get-tuple-element.35), channel_id=1, replica_groups=mesh['gx'=4,'gy'=8] {'gx','gy'}, dimensions={0} | all-to-all | bytes 32768 | tf_op jit(solution)/shard_map/all_to_all | solution.py:252
  72.1 0.0 copy-done.4
  72.1 0.9 %last.1 = (f32[8,128]{1,0:T(8,128)}, f32[8,128]{1,0:T(8,128)}, f32[5,4]{1,0:T(8,128)S(1)}) custom-call(f32[32,1,1,128]{3,2,1,0:T(1,128)S(1)} %all_to_all.34.recv, f32[8,128]{1,0:T(8,128)S(1)} %bitcast.14, f32[8,128]{1,0:T(8,128)S(1)} %get-tuple-element.25.refs_0_.start, f32[8,128]{1,0:T(8,128)S(1)} %get-tuple-element.27.refs_1_.refs_0_, ...), custom_call_target="tpu_custom_call" | custom-call | tf_op jit(solution)/shard_map/last/pallas_call | solution.py:291
  73.0 0.7 copy.8
  (5 shorter events, 0.0 us)
Async XLA Ops:
  0.7 0.7 copy-start.2
  2.6 14.9 %all-to-all-start = ((f32[32,5,1,128]{3,2,1,0:T(1,128)}), f32[32,5,1,128]{3,2,1,0:T(1,128)S(1)}, u32[]{:S(2)}, u32[]{:S(2)}) async-start(f32[32,5,1,128]{3,2,1,0:T(1,128)} %first.1), calls=%async_computation | async-start | bytes 163840 | tf_op jit(solution)/shard_map/all_to_all | solution.py:252
  17.5 1.9 %copy-start = (f32[2,4,6,128,128]{4,3,2,1,0:T(8,128)S(1)}, f32[2,4,6,128,128]{4,3,2,1,0:T(8,128)}, u32[]{:S(2)}) copy-start(f32[2,4,6,128,128]{4,3,2,1,0:T(8,128)} %tiles.9) | copy-start | bytes 9437188
  19.4 0.7 copy-start.3
  20.1 0.7 copy-start.5
  20.7 10.3 %copy-start.1 = (f32[2,4,6,128,128]{4,3,2,1,0:T(8,128)S(1)}, f32[2,4,6,128,128]{4,3,2,1,0:T(8,128)}, u32[]{:S(2)}) copy-start(f32[2,4,6,128,128]{4,3,2,1,0:T(8,128)} %tiles.9) | copy-start | bytes 9437188
  51.8 20.4 %copy-start.4 = (f32[2,4,128]{2,1,0:T(4,128)S(1)}, f32[2,4,128]{2,1,0:T(4,128)}, u32[]{:S(2)}) copy-start(f32[2,4,128]{2,1,0:T(4,128)} %param.9) | copy-start | bytes 12292

commit v2 on v1

--- a/solution.py
+++ b/solution.py
@@ -23,6 +23,9 @@
         self.rows = max(self.rx, self.ry) + 1
         self.width = self.ry + 2
         self.zero = (self.rx + 2) * (self.ry + 2)
+        self.bits = self.zero.bit_length()
+        self.fields = 31 // self.bits
+        self.words = -(-self.slots // self.fields)
 
     def edge(self, dx, dy):
         xs = {-1: [0], 0: range(self.rx), 1: [self.rx - 1]}[dx]
@@ -35,25 +38,26 @@
         return [x * self.width + y for x in xs for y in ys]
 
 
-def neighbour(shape, ix, iy, dx, dy):
+def neighbour(shape, dx, dy):
+    ix, iy = lax.axis_index("gx"), lax.axis_index("gy")
     x, y = ix + dx, iy + dy
     inside = (x >= 0) & (x < shape.nx) & (y >= 0) & (y < shape.ny)
     return jnp.where(inside, x * shape.ny + y, ix * shape.ny + iy)
 
 
-def pack(shape, here, rows, send):
+def pack(shape, rows, send):
     for dx, dy in OFFSETS:
-        dst = neighbour(shape, here[0], here[1], dx, dy)
+        dst = neighbour(shape, dx, dy)
         for k, (x, y) in enumerate(shape.edge(dx, dy)):
             send[dst, k] = rows[x * shape.ry + y]
 
 
-def unpack(shape, here, recv, own, padded):
+def unpack(shape, recv, own, padded):
     for x in range(shape.rx):
         for y in range(shape.ry):
             padded[(x + 1) * shape.width + y + 1] = own[x * shape.ry + y]
     for dx, dy in OFFSETS:
-        src = neighbour(shape, here[0], here[1], dx, dy)
+        src = neighbour(shape, dx, dy)
         for k, position in enumerate(shape.halo(dx, dy)):
             padded[position] = recv[src, k]
     padded[shape.zero] = jnp.zeros_like(padded[shape.zero])
@@ -65,11 +69,14 @@
         jnp.int32, (blk, blk), 1
     )
     out = []
+    words = [[index[b : b + 1, w : w + 1][0, 0] for w in range(shape.words)] for b in range(shape.nb)]
     for b in range(shape.nb):
         x, y = divmod(b, shape.ry)
         total = None
         for s in range(shape.slots):
-            term = tiles[x, y, s] * padded[index[b, s]]
+            word, place = divmod(s, shape.fields)
+            row = (words[b][word] >> (place * shape.bits)) & ((1 << shape.bits) - 1)
+            term = tiles[x, y, s] * padded[row]
             total = term if total is None else total + term
         column = jnp.sum(total, axis=1, keepdims=True)
         out.append(jnp.sum(jnp.where(eye, column, 0.0), axis=0, keepdims=True))
@@ -106,23 +113,29 @@
     return [value[b : b + 1] for b in range(value.shape[0])]
 
 
-def first_kernel(shape, here, guess, send):
+def first_kernel(shape, guess, send):
     rows = [guess[b : b + 1, :] for b in range(shape.nb)]
-    pack(shape, here, rows, send)
-
-
-def start_kernel(shape, here, index, tiles, recv, guess, right, send, start, padded):
-    unpack(shape, here, recv, [guess[b : b + 1, :] for b in range(shape.nb)], padded)
+    pack(shape, rows, send)
+
+
+def hold_kernel(*refs):
+    half = len(refs) // 2
+    for source, target in zip(refs[:half], refs[half:]):
+        target[...] = source[...]
+
+
+def start_kernel(shape, index, tiles, recv, guess, right, send, start, padded):
+    unpack(shape, recv, [guess[b : b + 1, :] for b in range(shape.nb)], padded)
     r = right[...] - matvec(shape, index, tiles, padded)
     start[...] = r
-    pack(shape, here, split(r), send)
+    pack(shape, split(r), send)
     send_dots(shape, spread([inner(r, r)]), send)
 
 
-def step_kernel(shape, step, here, index, tiles, recv, *refs):
+def step_kernel(shape, step, index, tiles, recv, *refs):
     keep, (send, v_out, w_out, *h_out, padded) = refs[: 2 * step + 1], refs[2 * step + 1 :]
     last = keep[-1]
-    unpack(shape, here, recv, split(last[...]), padded)
+    unpack(shape, recv, split(last[...]), padded)
     image = matvec(shape, index, tiles, padded)
     sums = sum_dots(shape, recv, shape.rows - 1, step + 1)
     square = sums[step]
@@ -150,7 +163,7 @@
     w_out[...] = w
     h_out[0][...] = spread(sums[:step] + [length])
     if step + 1 < ITERS:
-        pack(shape, here, split(w), send)
+        pack(shape, split(w), send)
     dots = [inner(w, other) for other in basis + [v, w]]
     row = spread(dots)
     if step + 1 < ITERS:
@@ -176,9 +189,8 @@
     for j in range(1, ITERS):
         columns.append([hs[j][:, i : i + 1] for i in range(j + 1)])
     columns.append(sums[:ITERS] + [jnp.sqrt(square)])
-    hess[...] = jnp.zeros_like(hess)
-    row = lax.broadcasted_iota(jnp.int32, hess.shape, 0)
-    col = lax.broadcasted_iota(jnp.int32, hess.shape, 1)
+    row = lax.broadcasted_iota(jnp.int32, hess.shape, 1)
+    col = lax.broadcasted_iota(jnp.int32, hess.shape, 0)
     full = jnp.zeros(hess.shape, jnp.float32)
     for j, column in enumerate(columns):
         for i, value in enumerate(column):
@@ -222,25 +234,28 @@
     residual[...] = r
 
 
-def table(shape, here, codes, counts):
+def table(shape, codes, counts):
     x = jnp.arange(shape.rx, dtype=jnp.int32)[:, None, None] + codes // 3
     y = jnp.arange(shape.ry, dtype=jnp.int32)[None, :, None] + codes % 3
-    gx = here[0] * shape.rx + x - 1
-    gy = here[1] * shape.ry + y - 1
+    gx = lax.axis_index("gx") * shape.rx + x - 1
+    gy = lax.axis_index("gy") * shape.ry + y - 1
     live = jnp.arange(shape.slots, dtype=jnp.int32) < counts[:, :, None]
     live &= (gx >= 0) & (gx < shape.nx * shape.rx) & (gy >= 0) & (gy < shape.ny * shape.ry)
-    return jnp.where(live, x * shape.width + y, shape.zero).reshape(shape.nb, shape.slots)
+    place = jnp.where(live, x * shape.width + y, shape.zero).reshape(shape.nb, shape.slots)
+    words = [
+        sum(place[:, s] << ((s % shape.fields) * shape.bits) for s in range(shape.slots) if s // shape.fields == w)
+        for w in range(shape.words)
+    ]
+    return jnp.stack(words, axis=1)
 
 
 def body(tiles, codes, counts, right_side, initial_guess):
     shape = Shape(codes)
     blk = tiles.shape[-1]
-    here = jnp.stack([lax.axis_index("gx"), lax.axis_index("gy")]).astype(jnp.int32)
-    index = table(shape, here, codes, counts)
+    index = table(shape, codes, counts)
     flat = (shape.nb, blk)
     guess = initial_guess.reshape(flat)
     right = right_side.reshape(flat)
-    smem = pl.BlockSpec(memory_space=pltpu.SMEM)
     vmem = pl.BlockSpec(memory_space=pltpu.VMEM)
     vector = jax.ShapeDtypeStruct(flat, jnp.float32)
     small = jax.ShapeDtypeStruct((1, blk), jnp.float32)
@@ -254,21 +269,30 @@
     send = pl.pallas_call(
         functools.partial(first_kernel, shape),
         out_shape=buffer,
-        in_specs=[smem, vmem],
+        in_specs=[vmem],
         out_specs=vmem,
         compiler_params=params,
         name="first",
-    )(here, guess)
+    )(guess)
     recv = exchange(send)
+    tiles, guess, right = pl.pallas_call(
+        hold_kernel,
+        out_shape=(jax.ShapeDtypeStruct(tiles.shape, jnp.float32), vector, vector),
+        in_specs=[vmem] * 3,
+        out_specs=(vmem,) * 3,
+        compiler_params=params,
+        cost_estimate=pl.CostEstimate(flops=10_000_000, bytes_accessed=0, transcendentals=0),
+        name="hold",
+    )(tiles, guess, right)
     send, start = pl.pallas_call(
         functools.partial(start_kernel, shape),
         out_shape=(buffer, vector),
-        in_specs=[smem, smem, vmem, vmem, vmem, vmem],
+        in_specs=[vmem] * 5,
         out_specs=(vmem, vmem),
         scratch_shapes=[padded],
         compiler_params=params,
         name="start",
-    )(here, index, tiles, recv, guess, right)
+    )(index, tiles, recv, guess, right)
     vs, ws, hs = [], [], []
     for step in range(ITERS):
         recv = exchange(send)
@@ -278,26 +302,26 @@
         send, v, w, h = pl.pallas_call(
             functools.partial(step_kernel, shape, step),
             out_shape=(out, vector, vector, small),
-            in_specs=[smem, smem] + [vmem] * (2 + len(keep)),
+            in_specs=[vmem] * (3 + len(keep)),
             out_specs=(vmem,) * 4,
             scratch_shapes=[padded],
             compiler_params=params,
             name=f"step{step}",
-        )(here, index, tiles, recv, *keep)
+        )(index, tiles, recv, *keep)
         vs.append(v)
         ws.append(w)
         hs.append(h)
     recv = exchange(send)
     solution, residual, hessenberg = pl.pallas_call(
         functools.partial(last_kernel, shape),
-        out_shape=(vector, vector, jax.ShapeDtypeStruct((ITERS + 1, ITERS), jnp.float32)),
+        out_shape=(vector, vector, jax.ShapeDtypeStruct((ITERS, ITERS + 1), jnp.float32)),
         in_specs=[vmem] * (3 + 3 * ITERS),
         out_specs=(vmem,) * 3,
         compiler_params=params,
         name="last",
     )(recv, guess, start, *vs, *ws, *hs)
     whole = initial_guess.shape
-    return solution.reshape(whole), residual.reshape(whole), hessenberg
+    return solution.reshape(whole), residual.reshape(whole), hessenberg.T
 
 
 def solution(mesh):

time: 74.1 us -> 66.5 us (0.90)
  Pallas kernels: 7.55 us -> 4.2 us
  waiting for transfers between devices: 6.77 us -> 3.89 us
    all_to_all x1, waiting for transfers between devices: 6.77 us -> 3.89 us  [exchange(): return lax.all_to_all(send, AXES, 0, 0, tiled=True)]
    pallas_call x4, Pallas kernels: 4.41 us -> 2.01 us  [body(): pl.pallas_call(functools.partial(step_kernel, shape, step), out_shape=(ou...]
    unnamed x13 -> x12, local copies, waits for them, and re-layouts: 4.62 us -> 3.95 us
  transfers between devices with their start and end apart: 1 -> 1, of which waited for: 1 -> 1; matrix products, arithmetic and copies ran while one was open for 1% -> 0% of each run, Pallas kernels for 0% -> 0%
where the time goes in v2:
time: 66.5 us; the launch traced here: 66.2 us
  blocking collectives  45.9 us (69%)
  starting transfers between devices  7.33 us (11%)
  Pallas kernels  4.2 us (6%)
  local copies, waits for them, and re-layouts  3.95 us (6%)
  waiting for transfers between devices  3.89 us (6%)
  between operations  0.73 us (1%)
    all_to_all x5, blocking collectives, exchange(): return lax.all_to_all(send, AXES, 0, 0, tiled=True)  45.9 us
    all_to_all x1, starting transfers between devices, exchange(): return lax.all_to_all(send, AXES, 0, 0, tiled=True)  7.33 us
    unnamed x12, local copies, waits for them, and re-layouts  3.95 us
    all_to_all x1, waiting for transfers between devices, exchange(): return lax.all_to_all(send, AXES, 0, 0, tiled=True)  3.89 us
    pallas_call x4, Pallas kernels, body(): pl.pallas_call(functools.partial(step_kernel, shape, step), out_shape=(ou...  2.01 us
  transfers between devices with their start and end apart: 1, of which 1 were waited for; matrix products, arithmetic and copies ran while one was open for 0% of the time, Pallas kernels for 0%

profile of v2, /device:TPU:0, one launch (start us, length us, event | category | flops | bytes accessed | tf_op | source)
XLA Modules:
  0.0 66.2 jit_solution(2724403304645198725)
XLA Ops:
  0.6 0.0 copy-start.1
  0.7 0.7 %copy-done.1 = f32[2,4,128]{2,1,0:T(4,128)S(1)} copy-done((f32[2,4,128]{2,1,0:T(4,128)S(1)}, f32[2,4,128]{2,1,0:T(4,128)}, u32[]{:S(2)}) %copy-start.1) | copy-done | bytes 4120
  1.3 0.6 first.1
  2.0 7.3 %all-to-all-start = ((f32[32,5,1,128]{3,2,1,0:T(1,128)}), f32[32,5,1,128]{3,2,1,0:T(1,128)S(1)}, u32[]{:S(2)}, u32[]{:S(2)}) async-start(f32[32,5,1,128]{3,2,1,0:T(1,128)} %first.1), calls=%async_computation | async-start | bytes 163840 | tf_op jit(solution)/shard_map/all_to_all | solution.py:267
  9.3 0.0 copy-start
  9.3 1.9 %copy-done = f32[2,4,6,128,128]{4,3,2,1,0:T(8,128)S(1)} copy-done((f32[2,4,6,128,128]{4,3,2,1,0:T(8,128)S(1)}, f32[2,4,6,128,128]{4,3,2,1,0:T(8,128)}, u32[]{:S(2)}) %copy-start) | copy-done | bytes 3145752
  11.2 0.7 %copy-done.2 = f32[2,4,128]{2,1,0:T(4,128)S(1)} copy-done((f32[2,4,128]{2,1,0:T(4,128)S(1)}, f32[2,4,128]{2,1,0:T(4,128)}, u32[]{:S(2)}) %copy-start.2) | copy-done | bytes 4120
  11.9 0.7 %copy-done.3 = f32[2,4,128]{2,1,0:T(4,128)S(1)} copy-done((f32[2,4,128]{2,1,0:T(4,128)S(1)}, f32[2,4,128]{2,1,0:T(4,128)}, u32[]{:S(2)}) %copy-start.3) | copy-done | bytes 4120
  12.6 0.2 hold.1
  12.8 0.0 copy-done.5
  12.8 0.1 add_select_fusion.2
  12.9 0.1 shift-left_add_fusion.index
  13.0 3.9 %all-to-all-done.recv = f32[32,5,1,128]{3,2,1,0:T(1,128)S(1)} async-done(((f32[32,5,1,128]{3,2,1,0:T(1,128)}), f32[32,5,1,128]{3,2,1,0:T(1,128)S(1)}, u32[]{:S(2)}, u32[]{:S(2)}) %all-to-all-start) | async-done | bytes 81952 | tf_op jit(solution)/shard_map/all_to_all | solution.py:267
  16.8 0.5 start.1
  17.4 9.3 %all_to_all.30.recv = f32[32,5,1,128]{3,2,1,0:T(1,128)S(1)} all-to-all(f32[32,5,1,128]{3,2,1,0:T(1,128)S(1)} %get-tuple-element.30), channel_id=1, replica_groups=mesh['gx'=4,'gy'=8] {'gx','gy'}, dimensions={0} | all-to-all | bytes 163840 | tf_op jit(solution)/shard_map/all_to_all | solution.py:267
  26.7 0.5 step0.1
  27.1 9.2 %all_to_all.31.recv = f32[32,5,1,128]{3,2,1,0:T(1,128)S(1)} all-to-all(f32[32,5,1,128]{3,2,1,0:T(1,128)S(1)} %get-tuple-element.32), channel_id=1, replica_groups=mesh['gx'=4,'gy'=8] {'gx','gy'}, dimensions={0} | all-to-all | bytes 163840 | tf_op jit(solution)/shard_map/all_to_all | solution.py:267
  36.4 0.5 step1.1
  36.9 9.2 %all_to_all.32.recv = f32[32,5,1,128]{3,2,1,0:T(1,128)S(1)} all-to-all(f32[32,5,1,128]{3,2,1,0:T(1,128)S(1)} %get-tuple-element.35), channel_id=1, replica_groups=mesh['gx'=4,'gy'=8] {'gx','gy'}, dimensions={0} | all-to-all | bytes 163840 | tf_op jit(solution)/shard_map/all_to_all | solution.py:267
  46.2 0.5 step2.1
  46.7 9.2 %all_to_all.33.recv = f32[32,5,1,128]{3,2,1,0:T(1,128)S(1)} all-to-all(f32[32,5,1,128]{3,2,1,0:T(1,128)S(1)} %get-tuple-element.38), channel_id=1, replica_groups=mesh['gx'=4,'gy'=8] {'gx','gy'}, dimensions={0} | all-to-all | bytes 163840 | tf_op jit(solution)/shard_map/all_to_all | solution.py:267
  55.9 0.5 step3.1
  56.4 8.9 %all_to_all.34.recv = f32[32,1,1,128]{3,2,1,0:T(1,128)S(1)} all-to-all(f32[32,1,1,128]{3,2,1,0:T(1,128)S(1)} %get-tuple-element.41), channel_id=1, replica_groups=mesh['gx'=4,'gy'=8] {'gx','gy'}, dimensions={0} | all-to-all | bytes 32768 | tf_op jit(solution)/shard_map/all_to_all | solution.py:267
  65.3 0.9 %last.1 = (f32[8,128]{1,0:T(8,128)}, f32[8,128]{1,0:T(8,128)}, f32[4,5]{1,0:T(4,128)}) custom-call(f32[32,1,1,128]{3,2,1,0:T(1,128)S(1)} %all_to_all.34.recv, f32[8,128]{1,0:T(8,128)S(1)} %get-tuple-element.28.guess, f32[8,128]{1,0:T(8,128)S(1)} %get-tuple-element.31.refs_0_.start, f32[8,128]{1,0:T(8,128)S(1)} %get-tuple-element.33.refs_1_.refs_0_, ...), custom_call_target="tpu_custom_call" | custom-call | tf_op jit(solution)/shard_map/last/pallas_call | solution.py:315
  (5 shorter events, 0.0 us)
Async XLA Ops:
  0.6 12.1 %copy-start.5 = (s32[2,4]{1,0:T(2,128)S(1)}, s32[2,4]{1,0:T(2,128)}, u32[]{:S(2)}) copy-start(s32[2,4]{1,0:T(2,128)} %param.7) | copy-start | bytes 100
  0.6 0.7 %copy-start.1 = (f32[2,4,128]{2,1,0:T(4,128)S(1)}, f32[2,4,128]{2,1,0:T(4,128)}, u32[]{:S(2)}) copy-start(f32[2,4,128]{2,1,0:T(4,128)} %param.9) | copy-start | bytes 12292
  1.3 11.5 %copy-start.4 = (s32[2,4,6]{2,1,0:T(4,128)S(1)}, s32[2,4,6]{2,1,0:T(4,128)}, u32[]{:S(2)}) copy-start(s32[2,4,6]{2,1,0:T(4,128)} %param.6) | copy-start | bytes 580
  2.0 14.9 %all-to-all-start = ((f32[32,5,1,128]{3,2,1,0:T(1,128)}), f32[32,5,1,128]{3,2,1,0:T(1,128)S(1)}, u32[]{:S(2)}, u32[]{:S(2)}) async-start(f32[32,5,1,128]{3,2,1,0:T(1,128)} %first.1), calls=%async_computation | async-start | bytes 163840 | tf_op jit(solution)/shard_map/all_to_all | solution.py:267
  9.3 1.9 %copy-start = (f32[2,4,6,128,128]{4,3,2,1,0:T(8,128)S(1)}, f32[2,4,6,128,128]{4,3,2,1,0:T(8,128)}, u32[]{:S(2)}) copy-start(f32[2,4,6,128,128]{4,3,2,1,0:T(8,128)} %refs_0_.1) | copy-start | bytes 9437188
  11.2 0.7 %copy-start.2 = (f32[2,4,128]{2,1,0:T(4,128)S(1)}, f32[2,4,128]{2,1,0:T(4,128)}, u32[]{:S(2)}) copy-start(f32[2,4,128]{2,1,0:T(4,128)} %param.9) | copy-start | bytes 12292
  11.9 0.7 %copy-start.3 = (f32[2,4,128]{2,1,0:T(4,128)S(1)}, f32[2,4,128]{2,1,0:T(4,128)}, u32[]{:S(2)}) copy-start(f32[2,4,128]{2,1,0:T(4,128)} %param.8) | copy-start | bytes 12292

commit v3 on v2

--- a/solution.py
+++ b/solution.py
@@ -24,7 +24,7 @@
         self.width = self.ry + 2
         self.zero = (self.rx + 2) * (self.ry + 2)
         self.bits = self.zero.bit_length()
-        self.fields = 31 // self.bits
+        self.fields = 24 // self.bits
         self.words = -(-self.slots // self.fields)
 
     def edge(self, dx, dy):
@@ -61,6 +61,31 @@
         for k, position in enumerate(shape.halo(dx, dy)):
             padded[position] = recv[src, k]
     padded[shape.zero] = jnp.zeros_like(padded[shape.zero])
+
+
+def table(shape, codes, counts, index):
+    size = (shape.ry, shape.slots)
+    slot = lax.broadcasted_iota(jnp.int32, size, 1)
+    square = (shape.ry, shape.ry)
+    eye = lax.broadcasted_iota(jnp.int32, square, 0) == lax.broadcasted_iota(jnp.int32, square, 1)
+    for x in range(shape.rx):
+        code = codes[x]
+        row = counts[x : x + 1, :].astype(jnp.float32)
+        count = jnp.sum(jnp.where(eye, row, 0.0), axis=1, keepdims=True).astype(jnp.int32)
+        down = jnp.where(code >= 6, 2, jnp.where(code >= 3, 1, 0))
+        px = x + down
+        py = lax.broadcasted_iota(jnp.int32, size, 0) + code - 3 * down
+        gx = lax.axis_index("gx") * shape.rx + px - 1
+        gy = lax.axis_index("gy") * shape.ry + py - 1
+        live = slot < count
+        live &= (gx >= 0) & (gx < shape.nx * shape.rx) & (gy >= 0) & (gy < shape.ny * shape.ry)
+        place = jnp.where(live, px * shape.width + py, shape.zero).astype(jnp.float32)
+        for w in range(shape.words):
+            word = None
+            for s in range(w * shape.fields, min((w + 1) * shape.fields, shape.slots)):
+                field = place[:, s : s + 1] * float(1 << ((s % shape.fields) * shape.bits))
+                word = field if word is None else word + field
+            index[x * shape.ry : (x + 1) * shape.ry, w : w + 1] = word.astype(jnp.int32)
 
 
 def matvec(shape, index, tiles, padded):
@@ -113,18 +138,14 @@
     return [value[b : b + 1] for b in range(value.shape[0])]
 
 
-def first_kernel(shape, guess, send):
+def first_kernel(shape, guess, *refs):
+    send = refs[-1]
     rows = [guess[b : b + 1, :] for b in range(shape.nb)]
     pack(shape, rows, send)
 
 
-def hold_kernel(*refs):
-    half = len(refs) // 2
-    for source, target in zip(refs[:half], refs[half:]):
-        target[...] = source[...]
-
-
-def start_kernel(shape, index, tiles, recv, guess, right, send, start, padded):
+def start_kernel(shape, codes, counts, tiles, recv, guess, right, send, start, index, padded):
+    table(shape, codes, counts, index)
     unpack(shape, recv, [guess[b : b + 1, :] for b in range(shape.nb)], padded)
     r = right[...] - matvec(shape, index, tiles, padded)
     start[...] = r
@@ -234,25 +255,9 @@
     residual[...] = r
 
 
-def table(shape, codes, counts):
-    x = jnp.arange(shape.rx, dtype=jnp.int32)[:, None, None] + codes // 3
-    y = jnp.arange(shape.ry, dtype=jnp.int32)[None, :, None] + codes % 3
-    gx = lax.axis_index("gx") * shape.rx + x - 1
-    gy = lax.axis_index("gy") * shape.ry + y - 1
-    live = jnp.arange(shape.slots, dtype=jnp.int32) < counts[:, :, None]
-    live &= (gx >= 0) & (gx < shape.nx * shape.rx) & (gy >= 0) & (gy < shape.ny * shape.ry)
-    place = jnp.where(live, x * shape.width + y, shape.zero).reshape(shape.nb, shape.slots)
-    words = [
-        sum(place[:, s] << ((s % shape.fields) * shape.bits) for s in range(shape.slots) if s // shape.fields == w)
-        for w in range(shape.words)
-    ]
-    return jnp.stack(words, axis=1)
-
-
 def body(tiles, codes, counts, right_side, initial_guess):
     shape = Shape(codes)
     blk = tiles.shape[-1]
-    index = table(shape, codes, counts)
     flat = (shape.nb, blk)
     guess = initial_guess.reshape(flat)
     right = right_side.reshape(flat)
@@ -268,31 +273,22 @@
 
     send = pl.pallas_call(
         functools.partial(first_kernel, shape),
-        out_shape=buffer,
-        in_specs=[vmem],
+        out_shape=jax.ShapeDtypeStruct((shape.nd, shape.rows - 1, 1, blk), jnp.float32),
+        in_specs=[vmem] + [pl.BlockSpec(memory_space=pltpu.HBM)] * 4,
         out_specs=vmem,
         compiler_params=params,
         name="first",
-    )(guess)
+    )(guess, *(pltpu.with_memory_space_constraint(x, pltpu.HBM) for x in (tiles, right, codes, counts)))
     recv = exchange(send)
-    tiles, guess, right = pl.pallas_call(
-        hold_kernel,
-        out_shape=(jax.ShapeDtypeStruct(tiles.shape, jnp.float32), vector, vector),
-        in_specs=[vmem] * 3,
+    send, start, index = pl.pallas_call(
+        functools.partial(start_kernel, shape),
+        out_shape=(buffer, vector, jax.ShapeDtypeStruct((shape.nb, shape.words), jnp.int32)),
+        in_specs=[vmem] * 6,
         out_specs=(vmem,) * 3,
-        compiler_params=params,
-        cost_estimate=pl.CostEstimate(flops=10_000_000, bytes_accessed=0, transcendentals=0),
-        name="hold",
-    )(tiles, guess, right)
-    send, start = pl.pallas_call(
-        functools.partial(start_kernel, shape),
-        out_shape=(buffer, vector),
-        in_specs=[vmem] * 5,
-        out_specs=(vmem, vmem),
         scratch_shapes=[padded],
         compiler_params=params,
         name="start",
-    )(index, tiles, recv, guess, right)
+    )(codes, counts, tiles, recv, guess, right)
     vs, ws, hs = [], [], []
     for step in range(ITERS):
         recv = exchange(send)

time: 66.5 us -> 66 us (level)
  blocking collectives: 45.9 us -> 60.4 us
  starting transfers between devices: 7.33 us -> 0 us
  waiting for transfers between devices: 3.89 us -> 0 us
  local copies, waits for them, and re-layouts: 3.95 us -> 0.85 us
    all_to_all x5 -> x6, blocking collectives: 45.9 us -> 60.4 us  [exchange(): return lax.all_to_all(send, AXES, 0, 0, tiled=True)]
    all_to_all x1 -> x0, starting transfers between devices: 7.33 us -> none  [exchange(): return lax.all_to_all(send, AXES, 0, 0, tiled=True)]
    all_to_all x1 -> x0, waiting for transfers between devices: 3.89 us -> none  [exchange(): return lax.all_to_all(send, AXES, 0, 0, tiled=True)]
    unnamed x12 -> x10, local copies, waits for them, and re-layouts: 3.95 us -> 0.85 us
    pallas_call x2 -> x1, Pallas kernels: 0.83 us -> 0.01 us  [body(): pl.pallas_call(functools.partial(first_kernel, shape), out_shape=jax.Shap...]
  transfers between devices with their start and end apart: 1 -> 0, of which waited for: 1 -> 0; matrix products, arithmetic and copies ran while one was open for 0% -> 0% of each run, Pallas kernels for 0% -> 0%
where the time goes in v3:
time: 66 us; the launch traced here: 65.7 us
  blocking collectives  60.4 us (92%)
  Pallas kernels  3.8 us (6%)
  local copies, waits for them, and re-layouts  0.85 us (1%)
  between operations  0.71 us (1%)
    all_to_all x6, blocking collectives, exchange(): return lax.all_to_all(send, AXES, 0, 0, tiled=True)  60.4 us
    pallas_call x4, Pallas kernels, body(): pl.pallas_call(functools.partial(step_kernel, shape, step), out_shape=(ou...  2.19 us

profile of v3, /device:TPU:0, one launch (start us, length us, event | category | flops | bytes accessed | tf_op | source)
XLA Modules:
  0.0 65.7 jit_solution(11684587759078665357)
XLA Ops:
  0.6 0.0 copy-start
  0.6 0.0 copy-start.1
  0.7 0.8 %copy-done.1 = f32[2,4,128]{2,1,0:T(4,128)S(1)} copy-done((f32[2,4,128]{2,1,0:T(4,128)S(1)}, f32[2,4,128]{2,1,0:T(4,128)}, u32[]{:S(2)}) %copy-start.1) | copy-done | bytes 4120
  1.5 0.0 copy-start.2
  1.5 0.0 copy-start.3
  1.5 0.0 copy-start.4
  1.5 14.5 %all_to_all.30.recv = f32[32,4,1,128]{3,2,1,0:T(1,128)S(1)} all-to-all(f32[32,4,1,128]{3,2,1,0:T(1,128)S(1)} %first.1), channel_id=1, replica_groups=mesh['gx'=4,'gy'=8] {'gx','gy'}, dimensions={0} | all-to-all | bytes 131072 | tf_op jit(solution)/shard_map/all_to_all | solution.py:272
  16.0 0.0 copy-done
  16.0 0.0 copy-done.2
  16.0 0.0 copy-done.3
  16.0 0.0 copy-done.4
  16.0 0.7 %start.1 = (f32[32,5,1,128]{3,2,1,0:T(1,128)S(1)}, f32[8,128]{1,0:T(8,128)S(1)}, s32[8,2]{1,0:T(8,128)S(1)}) custom-call(s32[2,4,6]{2,1,0:T(4,128)S(1)} %copy-done.2, s32[2,4]{1,0:T(2,128)S(1)} %copy-done.4, f32[2,4,6,128,128]{4,3,2,1,0:T(8,128)S(1)} %copy-done, f32[32,4,1,128]{3,2,1,0:T(1,128)S(1)} %all_to_all.30.recv, f32[8,128]{1,0:T(8,128)S(1)} %bitcast.6, ...), custom_call_target="tpu_custom_call" | custom-call | tf_op jit(solution)/shard_map/start/pallas_call | solution.py:283
  16.8 9.2 %all_to_all.31.recv = f32[32,5,1,128]{3,2,1,0:T(1,128)S(1)} all-to-all(f32[32,5,1,128]{3,2,1,0:T(1,128)S(1)} %get-tuple-element.26), channel_id=1, replica_groups=mesh['gx'=4,'gy'=8] {'gx','gy'}, dimensions={0} | all-to-all | bytes 163840 | tf_op jit(solution)/shard_map/all_to_all | solution.py:272
  26.0 0.5 step0.1
  26.6 9.2 %all_to_all.32.recv = f32[32,5,1,128]{3,2,1,0:T(1,128)S(1)} all-to-all(f32[32,5,1,128]{3,2,1,0:T(1,128)S(1)} %get-tuple-element.28), channel_id=1, replica_groups=mesh['gx'=4,'gy'=8] {'gx','gy'}, dimensions={0} | all-to-all | bytes 163840 | tf_op jit(solution)/shard_map/all_to_all | solution.py:272
  35.8 0.6 step1.1
  36.4 9.2 %all_to_all.33.recv = f32[32,5,1,128]{3,2,1,0:T(1,128)S(1)} all-to-all(f32[32,5,1,128]{3,2,1,0:T(1,128)S(1)} %get-tuple-element.31), channel_id=1, replica_groups=mesh['gx'=4,'gy'=8] {'gx','gy'}, dimensions={0} | all-to-all | bytes 163840 | tf_op jit(solution)/shard_map/all_to_all | solution.py:272
  45.6 0.5 step2.1
  46.2 9.2 %all_to_all.34.recv = f32[32,5,1,128]{3,2,1,0:T(1,128)S(1)} all-to-all(f32[32,5,1,128]{3,2,1,0:T(1,128)S(1)} %get-tuple-element.34), channel_id=1, replica_groups=mesh['gx'=4,'gy'=8] {'gx','gy'}, dimensions={0} | all-to-all | bytes 163840 | tf_op jit(solution)/shard_map/all_to_all | solution.py:272
  55.4 0.5 step3.1
  56.0 8.9 %all_to_all.35.recv = f32[32,1,1,128]{3,2,1,0:T(1,128)S(1)} all-to-all(f32[32,1,1,128]{3,2,1,0:T(1,128)S(1)} %get-tuple-element.37), channel_id=1, replica_groups=mesh['gx'=4,'gy'=8] {'gx','gy'}, dimensions={0} | all-to-all | bytes 32768 | tf_op jit(solution)/shard_map/all_to_all | solution.py:272
  64.9 0.9 %last.1 = (f32[8,128]{1,0:T(8,128)}, f32[8,128]{1,0:T(8,128)}, f32[4,5]{1,0:T(4,128)}) custom-call(f32[32,1,1,128]{3,2,1,0:T(1,128)S(1)} %all_to_all.35.recv, f32[8,128]{1,0:T(8,128)S(1)} %bitcast.7, f32[8,128]{1,0:T(8,128)S(1)} %get-tuple-element.27.refs_0_.start, f32[8,128]{1,0:T(8,128)S(1)} %get-tuple-element.29.refs_1_.refs_0_, ...), custom_call_target="tpu_custom_call" | custom-call | tf_op jit(solution)/shard_map/last/pallas_call | solution.py:311
  (1 shorter events, 0.0 us)
Async XLA Ops:
  0.6 15.4 %copy-start = (f32[2,4,6,128,128]{4,3,2,1,0:T(8,128)S(1)}, f32[2,4,6,128,128]{4,3,2,1,0:T(8,128)}, u32[]{:S(2)}) copy-start(f32[2,4,6,128,128]{4,3,2,1,0:T(8,128)} %tiles.9) | copy-start | bytes 9437188
  0.6 0.8 %copy-start.1 = (f32[2,4,128]{2,1,0:T(4,128)S(1)}, f32[2,4,128]{2,1,0:T(4,128)}, u32[]{:S(2)}) copy-start(f32[2,4,128]{2,1,0:T(4,128)} %param.9) | copy-start | bytes 12292
  1.5 14.6 %copy-start.2 = (s32[2,4,6]{2,1,0:T(4,128)S(1)}, s32[2,4,6]{2,1,0:T(4,128)}, u32[]{:S(2)}) copy-start(s32[2,4,6]{2,1,0:T(4,128)} %codes.1) | copy-start | bytes 580
  1.5 14.6 %copy-start.3 = (f32[2,4,128]{2,1,0:T(4,128)S(1)}, f32[2,4,128]{2,1,0:T(4,128)}, u32[]{:S(2)}) copy-start(f32[2,4,128]{2,1,0:T(4,128)} %param.8) | copy-start | bytes 12292
  1.5 14.6 %copy-start.4 = (s32[2,4]{1,0:T(2,128)S(1)}, s32[2,4]{1,0:T(2,128)}, u32[]{:S(2)}) copy-start(s32[2,4]{1,0:T(2,128)} %counts.1) | copy-start | bytes 100

commit v4 on v3

--- a/solution.py
+++ b/solution.py
@@ -24,7 +24,7 @@
         self.width = self.ry + 2
         self.zero = (self.rx + 2) * (self.ry + 2)
         self.bits = self.zero.bit_length()
-        self.fields = 24 // self.bits
+        self.fields = 31 // self.bits
         self.words = -(-self.slots // self.fields)
 
     def edge(self, dx, dy):
@@ -79,13 +79,14 @@
         gy = lax.axis_index("gy") * shape.ry + py - 1
         live = slot < count
         live &= (gx >= 0) & (gx < shape.nx * shape.rx) & (gy >= 0) & (gy < shape.ny * shape.ry)
-        place = jnp.where(live, px * shape.width + py, shape.zero).astype(jnp.float32)
+        place = jnp.where(live, px * shape.width + py, shape.zero)
+        place = place << (lax.rem(slot, shape.fields) * shape.bits)
         for w in range(shape.words):
             word = None
             for s in range(w * shape.fields, min((w + 1) * shape.fields, shape.slots)):
-                field = place[:, s : s + 1] * float(1 << ((s % shape.fields) * shape.bits))
-                word = field if word is None else word + field
-            index[x * shape.ry : (x + 1) * shape.ry, w : w + 1] = word.astype(jnp.int32)
+                field = place[:, s : s + 1]
+                word = field if word is None else word | field
+            index[x * shape.ry : (x + 1) * shape.ry, w : w + 1] = word
 
 
 def matvec(shape, index, tiles, padded):
@@ -104,7 +105,10 @@
             term = tiles[x, y, s] * padded[row]
             total = term if total is None else total + term
         column = jnp.sum(total, axis=1, keepdims=True)
-        out.append(jnp.sum(jnp.where(eye, column, 0.0), axis=0, keepdims=True))
+        row = jnp.zeros((8, blk), jnp.float32)
+        for k in range(0, blk, 8):
+            row = jnp.where(eye[k : k + 8], column[k : k + 8], row)
+        out.append(jnp.sum(row, axis=0, keepdims=True))
     return jnp.concatenate(out, axis=0)
 
 
@@ -150,48 +154,62 @@
     r = right[...] - matvec(shape, index, tiles, padded)
     start[...] = r
     pack(shape, split(r), send)
-    send_dots(shape, spread([inner(r, r)]), send)
+
+
+def first_step_kernel(shape, index, tiles, recv, start, send, image, padded):
+    r = start[...]
+    unpack(shape, recv, split(r), padded)
+    t = matvec(shape, index, tiles, padded)
+    image[...] = t
+    pack(shape, split(t), send)
+    send_dots(shape, spread([inner(r, r), inner(t, r), inner(t, t)]), send)
 
 
 def step_kernel(shape, step, index, tiles, recv, *refs):
-    keep, (send, v_out, w_out, *h_out, padded) = refs[: 2 * step + 1], refs[2 * step + 1 :]
-    last = keep[-1]
-    unpack(shape, recv, split(last[...]), padded)
+    count = 2 * step
+    keep, outs = refs[:count], list(refs[count:])
+    padded = outs.pop()
+    last = keep[-1][...]
+    unpack(shape, recv, split(last), padded)
     image = matvec(shape, index, tiles, padded)
-    sums = sum_dots(shape, recv, shape.rows - 1, step + 1)
-    square = sums[step]
-    if step == 0:
-        length = jnp.sqrt(square)
-        scale = 1.0 / length
-        v = last[...] * scale
-        w = image * scale
-        basis = []
+    if step == 1:
+        whole, cross, square = sum_dots(shape, recv, shape.rows - 1, 3)
+        beta = jnp.sqrt(whole)
+        inverse = 1.0 / beta
+        sums = [cross / whole]
+        square = square / whole
+        basis = [keep[0][...] * inverse]
+        images = [last * inverse]
+        image = image * inverse
     else:
-        for i in range(step):
-            square = square - sums[i] * sums[i]
-        length = jnp.sqrt(square)
-        scale = 1.0 / length
-        basis = [ref[...] for ref in keep[1 : step + 1]]
-        images = [ref[...] for ref in keep[step + 1 :]]
-        v = images[-1]
-        w = image
-        for i in range(step):
-            v = v - sums[i] * basis[i]
-            w = w - sums[i] * images[i]
-        v = v * scale
-        w = w * scale
-    v_out[...] = v
-    w_out[...] = w
-    h_out[0][...] = spread(sums[:step] + [length])
+        *sums, square = sum_dots(shape, recv, shape.rows - 1, step + 1)
+        basis = [ref[...] for ref in keep[:step]]
+        images = [ref[...] for ref in keep[step:]]
+    for value in sums:
+        square = square - value * value
+    length = jnp.sqrt(square)
+    scale = 1.0 / length
+    v, w = images[-1], image
+    for value, b, a in zip(sums, basis, images):
+        v = v - value * b
+        w = w - value * a
+    v = v * scale
+    w = w * scale
     if step + 1 < ITERS:
-        pack(shape, split(w), send)
-    dots = [inner(w, other) for other in basis + [v, w]]
-    row = spread(dots)
+        pack(shape, split(w), outs[0])
+    row = spread([inner(w, other) for other in basis + [v, w]])
     if step + 1 < ITERS:
-        send_dots(shape, row, send)
+        send_dots(shape, row, outs[0])
     else:
         for d in range(shape.nd):
-            send[d, 0] = row
+            outs[0][d, 0] = row
+    outs[1][...] = v
+    outs[2][...] = w
+    outs[3][...] = spread(sums + [length])
+    if step == 1:
+        outs[4][...] = basis[0]
+        outs[5][...] = images[0]
+        outs[6][...] = spread([beta])
 
 
 def last_kernel(shape, recv, guess, start, *refs):
@@ -265,6 +283,7 @@
     vector = jax.ShapeDtypeStruct(flat, jnp.float32)
     small = jax.ShapeDtypeStruct((1, blk), jnp.float32)
     buffer = jax.ShapeDtypeStruct((shape.nd, shape.rows, 1, blk), jnp.float32)
+    halo = jax.ShapeDtypeStruct((shape.nd, shape.rows - 1, 1, blk), jnp.float32)
     params = pltpu.CompilerParams(vmem_limit_bytes=VMEM_BYTES)
     padded = pltpu.VMEM((shape.zero + 1, 1, blk), jnp.float32)
 
@@ -273,7 +292,7 @@
 
     send = pl.pallas_call(
         functools.partial(first_kernel, shape),
-        out_shape=jax.ShapeDtypeStruct((shape.nd, shape.rows - 1, 1, blk), jnp.float32),
+        out_shape=halo,
         in_specs=[vmem] + [pl.BlockSpec(memory_space=pltpu.HBM)] * 4,
         out_specs=vmem,
         compiler_params=params,
@@ -282,28 +301,41 @@
     recv = exchange(send)
     send, start, index = pl.pallas_call(
         functools.partial(start_kernel, shape),
-        out_shape=(buffer, vector, jax.ShapeDtypeStruct((shape.nb, shape.words), jnp.int32)),
+        out_shape=(halo, vector, jax.ShapeDtypeStruct((shape.nb, shape.words), jnp.int32)),
         in_specs=[vmem] * 6,
         out_specs=(vmem,) * 3,
         scratch_shapes=[padded],
         compiler_params=params,
         name="start",
     )(codes, counts, tiles, recv, guess, right)
-    vs, ws, hs = [], [], []
-    for step in range(ITERS):
+    recv = exchange(send)
+    send, image = pl.pallas_call(
+        functools.partial(first_step_kernel, shape),
+        out_shape=(buffer, vector),
+        in_specs=[vmem] * 4,
+        out_specs=(vmem,) * 2,
+        scratch_shapes=[padded],
+        compiler_params=params,
+        name="step0",
+    )(index, tiles, recv, start)
+    vs, ws, hs = [start], [image], []
+    for step in range(1, ITERS):
         recv = exchange(send)
-        keep = [start, *vs, *ws]
         final = step + 1 == ITERS
         out = buffer if not final else jax.ShapeDtypeStruct((shape.nd, 1, 1, blk), jnp.float32)
-        send, v, w, h = pl.pallas_call(
+        more = (vector, vector, small) if step == 1 else ()
+        send, v, w, h, *more = pl.pallas_call(
             functools.partial(step_kernel, shape, step),
-            out_shape=(out, vector, vector, small),
-            in_specs=[vmem] * (3 + len(keep)),
-            out_specs=(vmem,) * 4,
+            out_shape=(out, vector, vector, small, *more),
+            in_specs=[vmem] * (3 + len(vs) + len(ws)),
+            out_specs=(vmem,) * (4 + len(more)),
             scratch_shapes=[padded],
             compiler_params=params,
             name=f"step{step}",
-        )(index, tiles, recv, *keep)
+        )(index, tiles, recv, *vs, *ws)
+        if step == 1:
+            v0, w0, beta = more
+            vs, ws, hs = [v0], [w0], [beta]
         vs.append(v)
         ws.append(w)
         hs.append(h)

time: 66 us -> 65.4 us (level)
    pallas_call x4 -> x3, Pallas kernels: 2.19 us -> 1.52 us  [body(): pl.pallas_call(functools.partial(step_kernel, shape, step), out_shape=(ou...]
where the time goes in v4:
time: 65.4 us; the launch traced here: 65.1 us
  blocking collectives  60.2 us (92%)
  Pallas kernels  3.38 us (5%)
  local copies, waits for them, and re-layouts  0.85 us (1%)
  between operations  0.72 us (1%)
    all_to_all x6, blocking collectives, exchange(): return lax.all_to_all(send, AXES, 0, 0, tiled=True)  60.2 us
    pallas_call x3, Pallas kernels, body(): pl.pallas_call(functools.partial(step_kernel, shape, step), out_shape=(ou...  1.52 us

profile of v4, /device:TPU:0, one launch (start us, length us, event | category | flops | bytes accessed | tf_op | source)
XLA Modules:
  0.0 65.1 jit_solution(4209040272269757839)
XLA Ops:
  0.6 0.0 copy-start
  0.6 0.0 copy-start.1
  0.7 0.8 %copy-done.1 = f32[2,4,128]{2,1,0:T(4,128)S(1)} copy-done((f32[2,4,128]{2,1,0:T(4,128)S(1)}, f32[2,4,128]{2,1,0:T(4,128)}, u32[]{:S(2)}) %copy-start.1) | copy-done | bytes 4120
  1.5 0.0 copy-start.2
  1.5 0.0 copy-start.3
  1.5 0.0 copy-start.4
  1.5 0.0 copy-start.5
  1.5 14.5 %all_to_all.30.recv = f32[32,4,1,128]{3,2,1,0:T(1,128)S(1)} all-to-all(f32[32,4,1,128]{3,2,1,0:T(1,128)S(1)} %first.1), channel_id=1, replica_groups=mesh['gx'=4,'gy'=8] {'gx','gy'}, dimensions={0} | all-to-all | bytes 131072 | tf_op jit(solution)/shard_map/all_to_all | solution.py:291
  16.1 0.0 copy-done
  16.1 0.0 copy-done.2
  16.1 0.0 copy-done.3
  16.1 0.0 copy-done.4
  16.1 0.0 copy-done.5
  16.1 0.5 start.1
  16.6 9.1 %all_to_all.31.recv = f32[32,4,1,128]{3,2,1,0:T(1,128)S(1)} all-to-all(f32[32,4,1,128]{3,2,1,0:T(1,128)S(1)} %get-tuple-element.27), channel_id=1, replica_groups=mesh['gx'=4,'gy'=8] {'gx','gy'}, dimensions={0} | all-to-all | bytes 131072 | tf_op jit(solution)/shard_map/all_to_all | solution.py:291
  25.7 0.5 step0.1
  26.1 9.2 %all_to_all.32.recv = f32[32,5,1,128]{3,2,1,0:T(1,128)S(1)} all-to-all(f32[32,5,1,128]{3,2,1,0:T(1,128)S(1)} %get-tuple-element.29), channel_id=1, replica_groups=mesh['gx'=4,'gy'=8] {'gx','gy'}, dimensions={0} | all-to-all | bytes 163840 | tf_op jit(solution)/shard_map/all_to_all | solution.py:291
  35.4 0.5 step1.1
  35.9 9.2 %all_to_all.33.recv = f32[32,5,1,128]{3,2,1,0:T(1,128)S(1)} all-to-all(f32[32,5,1,128]{3,2,1,0:T(1,128)S(1)} %get-tuple-element.31), channel_id=1, replica_groups=mesh['gx'=4,'gy'=8] {'gx','gy'}, dimensions={0} | all-to-all | bytes 163840 | tf_op jit(solution)/shard_map/all_to_all | solution.py:291
  45.1 0.5 step2.1
  45.7 9.2 %all_to_all.34.recv = f32[32,5,1,128]{3,2,1,0:T(1,128)S(1)} all-to-all(f32[32,5,1,128]{3,2,1,0:T(1,128)S(1)} %get-tuple-element.36), channel_id=1, replica_groups=mesh['gx'=4,'gy'=8] {'gx','gy'}, dimensions={0} | all-to-all | bytes 163840 | tf_op jit(solution)/shard_map/all_to_all | solution.py:291
  54.9 0.5 step3.1
  55.4 8.9 %all_to_all.35.recv = f32[32,1,1,128]{3,2,1,0:T(1,128)S(1)} all-to-all(f32[32,1,1,128]{3,2,1,0:T(1,128)S(1)} %get-tuple-element.39), channel_id=1, replica_groups=mesh['gx'=4,'gy'=8] {'gx','gy'}, dimensions={0} | all-to-all | bytes 32768 | tf_op jit(solution)/shard_map/all_to_all | solution.py:291
  64.3 0.9 %last.1 = (f32[8,128]{1,0:T(8,128)}, f32[8,128]{1,0:T(8,128)}, f32[4,5]{1,0:T(4,128)}) custom-call(f32[32,1,1,128]{3,2,1,0:T(1,128)S(1)} %all_to_all.35.recv, f32[8,128]{1,0:T(8,128)S(1)} %bitcast.7, f32[8,128]{1,0:T(8,128)S(1)} %get-tuple-element.28.start.refs_0_, f32[8,128]{1,0:T(8,128)S(1)} %get-tuple-element.32.refs_0_, ...), custom_call_target="tpu_custom_call" | custom-call | tf_op jit(solution)/shard_map/last/pallas_call | solution.py:343
  (1 shorter events, 0.0 us)
Async XLA Ops:
  0.6 15.4 %copy-start = (f32[2,4,6,128,128]{4,3,2,1,0:T(8,128)S(1)}, f32[2,4,6,128,128]{4,3,2,1,0:T(8,128)}, u32[]{:S(2)}) copy-start(f32[2,4,6,128,128]{4,3,2,1,0:T(8,128)} %tiles.9) | copy-start | bytes 9437188
  0.6 0.8 %copy-start.1 = (f32[2,4,128]{2,1,0:T(4,128)S(1)}, f32[2,4,128]{2,1,0:T(4,128)}, u32[]{:S(2)}) copy-start(f32[2,4,128]{2,1,0:T(4,128)} %param.9) | copy-start | bytes 12292
  1.5 14.6 %copy-start.2 = (f32[2,4,128]{2,1,0:T(4,128)S(1)}, f32[2,4,128]{2,1,0:T(4,128)}, u32[]{:S(2)}) copy-start(f32[2,4,128]{2,1,0:T(4,128)} %param.9) | copy-start | bytes 12292
  1.5 14.6 %copy-start.3 = (s32[2,4,6]{2,1,0:T(4,128)S(1)}, s32[2,4,6]{2,1,0:T(4,128)}, u32[]{:S(2)}) copy-start(s32[2,4,6]{2,1,0:T(4,128)} %codes.1) | copy-start | bytes 580
  1.5 14.6 %copy-start.4 = (f32[2,4,128]{2,1,0:T(4,128)S(1)}, f32[2,4,128]{2,1,0:T(4,128)}, u32[]{:S(2)}) copy-start(f32[2,4,128]{2,1,0:T(4,128)} %param.8) | copy-start | bytes 12292
  1.5 14.6 %copy-start.5 = (s32[2,4]{1,0:T(2,128)S(1)}, s32[2,4]{1,0:T(2,128)}, u32[]{:S(2)}) copy-start(s32[2,4]{1,0:T(2,128)} %counts.1) | copy-start | bytes 100

commit v5 on v4

--- a/solution.py
+++ b/solution.py
@@ -112,15 +112,23 @@
     return jnp.concatenate(out, axis=0)
 
 
+def single(row, i):
+    return row[:, i : i + 1]
+
+
+def lane(row, i):
+    return jnp.broadcast_to(row[:, i : i + 1], row.shape)
+
+
 def inner(a, b):
     return jnp.sum(jnp.sum(a * b, axis=1, keepdims=True), axis=0, keepdims=True)
 
 
 def spread(values):
-    lane = lax.broadcasted_iota(jnp.int32, (1, 128), 1)
+    place = lax.broadcasted_iota(jnp.int32, (1, 128), 1)
     row = jnp.zeros((1, 128), jnp.float32)
     for i, value in enumerate(values):
-        row = jnp.where(lane == i, value, row)
+        row = jnp.where(place == i, value, row)
     return row
 
 
@@ -129,13 +137,13 @@
         send[d, shape.rows - 1] = row
 
 
-def sum_dots(shape, recv, at, count):
+def sum_dots(shape, recv, at, count, pick):
     parts = [recv[d, at] for d in range(shape.nd)]
     while len(parts) > 1:
         parts = [a + b for a, b in zip(parts[::2], parts[1::2])] + (
             [parts[-1]] if len(parts) % 2 else []
         )
-    return [parts[0][:, i : i + 1] for i in range(count)]
+    return [pick(parts[0], i) for i in range(count)]
 
 
 def split(value):
@@ -173,7 +181,7 @@
     unpack(shape, recv, split(last), padded)
     image = matvec(shape, index, tiles, padded)
     if step == 1:
-        whole, cross, square = sum_dots(shape, recv, shape.rows - 1, 3)
+        whole, cross, square = sum_dots(shape, recv, shape.rows - 1, 3, single)
         beta = jnp.sqrt(whole)
         inverse = 1.0 / beta
         sums = [cross / whole]
@@ -182,7 +190,7 @@
         images = [last * inverse]
         image = image * inverse
     else:
-        *sums, square = sum_dots(shape, recv, shape.rows - 1, step + 1)
+        *sums, square = sum_dots(shape, recv, shape.rows - 1, step + 1, single)
         basis = [ref[...] for ref in keep[:step]]
         images = [ref[...] for ref in keep[step:]]
     for value in sums:
@@ -219,21 +227,21 @@
         refs[2 * ITERS : 3 * ITERS],
         refs[3 * ITERS :],
     )
-    sums = sum_dots(shape, recv, 0, ITERS + 1)
+    sums = sum_dots(shape, recv, 0, ITERS + 1, lane)
     square = sums[ITERS]
     for i in range(ITERS):
         square = square - sums[i] * sums[i]
     columns = []
-    beta = hs[0][:, 0:1]
+    beta = lane(hs[0][...], 0)
     for j in range(1, ITERS):
-        columns.append([hs[j][:, i : i + 1] for i in range(j + 1)])
+        columns.append([lane(hs[j][...], i) for i in range(j + 1)])
     columns.append(sums[:ITERS] + [jnp.sqrt(square)])
     row = lax.broadcasted_iota(jnp.int32, hess.shape, 1)
     col = lax.broadcasted_iota(jnp.int32, hess.shape, 0)
     full = jnp.zeros(hess.shape, jnp.float32)
     for j, column in enumerate(columns):
         for i, value in enumerate(column):
-            full = jnp.where((row == i) & (col == j), value, full)
+            full = jnp.where((row == i) & (col == j), value[:, :1], full)
     hess[...] = full
     normal = {}
     for a in range(ITERS):

time: 65.4 us -> 65.3 us (level)
  no operation moved by 1% of the time
where the time goes in v5:
time: 65.3 us; the launch traced here: 65 us
  blocking collectives  60.2 us (92%)
  Pallas kernels  3.24 us (5%)
  local copies, waits for them, and re-layouts  0.85 us (1%)
  between operations  0.72 us (1%)
    all_to_all x6, blocking collectives, exchange(): return lax.all_to_all(send, AXES, 0, 0, tiled=True)  60.2 us
    pallas_call x3, Pallas kernels, body(): pl.pallas_call(functools.partial(step_kernel, shape, step), out_shape=(ou...  1.51 us

profile of v5, /device:TPU:0, one launch (start us, length us, event | category | flops | bytes accessed | tf_op | source)
XLA Modules:
  0.0 65.0 jit_solution(1366692534641492138)
XLA Ops:
  0.6 0.0 copy-start
  0.6 0.0 copy-start.1
  0.7 0.8 %copy-done.1 = f32[2,4,128]{2,1,0:T(4,128)S(1)} copy-done((f32[2,4,128]{2,1,0:T(4,128)S(1)}, f32[2,4,128]{2,1,0:T(4,128)}, u32[]{:S(2)}) %copy-start.1) | copy-done | bytes 4120
  1.5 0.0 copy-start.2
  1.5 0.0 copy-start.3
  1.5 0.0 copy-start.4
  1.5 0.0 copy-start.5
  1.5 14.5 %all_to_all.30.recv = f32[32,4,1,128]{3,2,1,0:T(1,128)S(1)} all-to-all(f32[32,4,1,128]{3,2,1,0:T(1,128)S(1)} %first.1), channel_id=1, replica_groups=mesh['gx'=4,'gy'=8] {'gx','gy'}, dimensions={0} | all-to-all | bytes 131072 | tf_op jit(solution)/shard_map/all_to_all | solution.py:299
  16.1 0.0 copy-done
  16.1 0.0 copy-done.2
  16.1 0.0 copy-done.3
  16.1 0.0 copy-done.4
  16.1 0.0 copy-done.5
  16.1 0.5 start.1
  16.6 9.1 %all_to_all.31.recv = f32[32,4,1,128]{3,2,1,0:T(1,128)S(1)} all-to-all(f32[32,4,1,128]{3,2,1,0:T(1,128)S(1)} %get-tuple-element.27), channel_id=1, replica_groups=mesh['gx'=4,'gy'=8] {'gx','gy'}, dimensions={0} | all-to-all | bytes 131072 | tf_op jit(solution)/shard_map/all_to_all | solution.py:299
  25.7 0.5 step0.1
  26.1 9.2 %all_to_all.32.recv = f32[32,5,1,128]{3,2,1,0:T(1,128)S(1)} all-to-all(f32[32,5,1,128]{3,2,1,0:T(1,128)S(1)} %get-tuple-element.29), channel_id=1, replica_groups=mesh['gx'=4,'gy'=8] {'gx','gy'}, dimensions={0} | all-to-all | bytes 163840 | tf_op jit(solution)/shard_map/all_to_all | solution.py:299
  35.4 0.5 step1.1
  35.9 9.2 %all_to_all.33.recv = f32[32,5,1,128]{3,2,1,0:T(1,128)S(1)} all-to-all(f32[32,5,1,128]{3,2,1,0:T(1,128)S(1)} %get-tuple-element.31), channel_id=1, replica_groups=mesh['gx'=4,'gy'=8] {'gx','gy'}, dimensions={0} | all-to-all | bytes 163840 | tf_op jit(solution)/shard_map/all_to_all | solution.py:299
  45.1 0.5 step2.1
  45.6 9.2 %all_to_all.34.recv = f32[32,5,1,128]{3,2,1,0:T(1,128)S(1)} all-to-all(f32[32,5,1,128]{3,2,1,0:T(1,128)S(1)} %get-tuple-element.36), channel_id=1, replica_groups=mesh['gx'=4,'gy'=8] {'gx','gy'}, dimensions={0} | all-to-all | bytes 163840 | tf_op jit(solution)/shard_map/all_to_all | solution.py:299
  54.9 0.5 step3.1
  55.4 8.9 %all_to_all.35.recv = f32[32,1,1,128]{3,2,1,0:T(1,128)S(1)} all-to-all(f32[32,1,1,128]{3,2,1,0:T(1,128)S(1)} %get-tuple-element.39), channel_id=1, replica_groups=mesh['gx'=4,'gy'=8] {'gx','gy'}, dimensions={0} | all-to-all | bytes 32768 | tf_op jit(solution)/shard_map/all_to_all | solution.py:299
  64.3 0.7 %last.1 = (f32[8,128]{1,0:T(8,128)}, f32[8,128]{1,0:T(8,128)}, f32[4,5]{1,0:T(4,128)}) custom-call(f32[32,1,1,128]{3,2,1,0:T(1,128)S(1)} %all_to_all.35.recv, f32[8,128]{1,0:T(8,128)S(1)} %bitcast.7, f32[8,128]{1,0:T(8,128)S(1)} %get-tuple-element.28.start.refs_0_, f32[8,128]{1,0:T(8,128)S(1)} %get-tuple-element.32.refs_0_, ...), custom_call_target="tpu_custom_call" | custom-call | tf_op jit(solution)/shard_map/last/pallas_call | solution.py:351
  (1 shorter events, 0.0 us)
Async XLA Ops:
  0.6 15.4 %copy-start = (f32[2,4,6,128,128]{4,3,2,1,0:T(8,128)S(1)}, f32[2,4,6,128,128]{4,3,2,1,0:T(8,128)}, u32[]{:S(2)}) copy-start(f32[2,4,6,128,128]{4,3,2,1,0:T(8,128)} %tiles.9) | copy-start | bytes 9437188
  0.6 0.8 %copy-start.1 = (f32[2,4,128]{2,1,0:T(4,128)S(1)}, f32[2,4,128]{2,1,0:T(4,128)}, u32[]{:S(2)}) copy-start(f32[2,4,128]{2,1,0:T(4,128)} %param.9) | copy-start | bytes 12292
  1.5 14.6 %copy-start.2 = (f32[2,4,128]{2,1,0:T(4,128)S(1)}, f32[2,4,128]{2,1,0:T(4,128)}, u32[]{:S(2)}) copy-start(f32[2,4,128]{2,1,0:T(4,128)} %param.9) | copy-start | bytes 12292
  1.5 14.6 %copy-start.3 = (s32[2,4,6]{2,1,0:T(4,128)S(1)}, s32[2,4,6]{2,1,0:T(4,128)}, u32[]{:S(2)}) copy-start(s32[2,4,6]{2,1,0:T(4,128)} %codes.1) | copy-start | bytes 580
  1.5 14.6 %copy-start.4 = (f32[2,4,128]{2,1,0:T(4,128)S(1)}, f32[2,4,128]{2,1,0:T(4,128)}, u32[]{:S(2)}) copy-start(f32[2,4,128]{2,1,0:T(4,128)} %param.8) | copy-start | bytes 12292
  1.5 14.6 %copy-start.5 = (s32[2,4]{1,0:T(2,128)S(1)}, s32[2,4]{1,0:T(2,128)}, u32[]{:S(2)}) copy-start(s32[2,4]{1,0:T(2,128)} %counts.1) | copy-start | bytes 100

commit v6 on v5

--- a/solution.py
+++ b/solution.py
@@ -8,6 +8,7 @@
 from jax.sharding import PartitionSpec as P
 
 ITERS = 4
+SHIFT = 3.0
 AXES = ("gx", "gy")
 VMEM_BYTES = 12 * 1024 * 1024
 OFFSETS = [(dx, dy) for dx in (-1, 0, 1) for dy in (-1, 0, 1) if (dx, dy) != (0, 0)]
@@ -170,7 +171,8 @@
     t = matvec(shape, index, tiles, padded)
     image[...] = t
     pack(shape, split(t), send)
-    send_dots(shape, spread([inner(r, r), inner(t, r), inner(t, t)]), send)
+    u = t - SHIFT * r
+    send_dots(shape, spread([inner(r, r), inner(u, r), inner(u, u)]), send)
 
 
 def step_kernel(shape, step, index, tiles, recv, *refs):
@@ -195,6 +197,7 @@
         images = [ref[...] for ref in keep[step:]]
     for value in sums:
         square = square - value * value
+    sums[-1] = sums[-1] + SHIFT
     length = jnp.sqrt(square)
     scale = 1.0 / length
     v, w = images[-1], image
@@ -205,7 +208,8 @@
     w = w * scale
     if step + 1 < ITERS:
         pack(shape, split(w), outs[0])
-    row = spread([inner(w, other) for other in basis + [v, w]])
+    u = w - SHIFT * v
+    row = spread([inner(u, other) for other in basis + [v, u]])
     if step + 1 < ITERS:
         send_dots(shape, row, outs[0])
     else:
@@ -231,6 +235,7 @@
     square = sums[ITERS]
     for i in range(ITERS):
         square = square - sums[i] * sums[i]
+    sums[ITERS - 1] = sums[ITERS - 1] + SHIFT
     columns = []
     beta = lane(hs[0][...], 0)
     for j in range(1, ITERS):

time: 65.3 us -> 65.3 us (level)
  no operation moved by 1% of the time
where the time goes in v6:
time: 65.3 us; the launch traced here: 65 us
  blocking collectives  60.2 us (92%)
  Pallas kernels  3.26 us (5%)
  local copies, waits for them, and re-layouts  0.85 us (1%)
  between operations  0.72 us (1%)
    all_to_all x6, blocking collectives, exchange(): return lax.all_to_all(send, AXES, 0, 0, tiled=True)  60.2 us
    pallas_call x3, Pallas kernels, body(): pl.pallas_call(functools.partial(step_kernel, shape, step), out_shape=(ou...  1.52 us

profile of v6, /device:TPU:0, one launch (start us, length us, event | category | flops | bytes accessed | tf_op | source)
XLA Modules:
  0.0 65.0 jit_solution(11927091404826847030)
XLA Ops:
  0.6 0.0 copy-start
  0.6 0.0 copy-start.1
  0.7 0.8 %copy-done.1 = f32[2,4,128]{2,1,0:T(4,128)S(1)} copy-done((f32[2,4,128]{2,1,0:T(4,128)S(1)}, f32[2,4,128]{2,1,0:T(4,128)}, u32[]{:S(2)}) %copy-start.1) | copy-done | bytes 4120
  1.5 0.0 copy-start.2
  1.5 0.0 copy-start.3
  1.5 0.0 copy-start.4
  1.5 0.0 copy-start.5
  1.5 14.5 %all_to_all.30.recv = f32[32,4,1,128]{3,2,1,0:T(1,128)S(1)} all-to-all(f32[32,4,1,128]{3,2,1,0:T(1,128)S(1)} %first.1), channel_id=1, replica_groups=mesh['gx'=4,'gy'=8] {'gx','gy'}, dimensions={0} | all-to-all | bytes 131072 | tf_op jit(solution)/shard_map/all_to_all | solution.py:304
  16.1 0.0 copy-done
  16.1 0.0 copy-done.2
  16.1 0.0 copy-done.3
  16.1 0.0 copy-done.4
  16.1 0.0 copy-done.5
  16.1 0.5 start.1
  16.6 9.1 %all_to_all.31.recv = f32[32,4,1,128]{3,2,1,0:T(1,128)S(1)} all-to-all(f32[32,4,1,128]{3,2,1,0:T(1,128)S(1)} %get-tuple-element.27), channel_id=1, replica_groups=mesh['gx'=4,'gy'=8] {'gx','gy'}, dimensions={0} | all-to-all | bytes 131072 | tf_op jit(solution)/shard_map/all_to_all | solution.py:304
  25.7 0.5 step0.1
  26.1 9.2 %all_to_all.32.recv = f32[32,5,1,128]{3,2,1,0:T(1,128)S(1)} all-to-all(f32[32,5,1,128]{3,2,1,0:T(1,128)S(1)} %get-tuple-element.29), channel_id=1, replica_groups=mesh['gx'=4,'gy'=8] {'gx','gy'}, dimensions={0} | all-to-all | bytes 163840 | tf_op jit(solution)/shard_map/all_to_all | solution.py:304
  35.4 0.5 step1.1
  35.9 9.2 %all_to_all.33.recv = f32[32,5,1,128]{3,2,1,0:T(1,128)S(1)} all-to-all(f32[32,5,1,128]{3,2,1,0:T(1,128)S(1)} %get-tuple-element.31), channel_id=1, replica_groups=mesh['gx'=4,'gy'=8] {'gx','gy'}, dimensions={0} | all-to-all | bytes 163840 | tf_op jit(solution)/shard_map/all_to_all | solution.py:304
  45.2 0.5 step2.1
  45.7 9.2 %all_to_all.34.recv = f32[32,5,1,128]{3,2,1,0:T(1,128)S(1)} all-to-all(f32[32,5,1,128]{3,2,1,0:T(1,128)S(1)} %get-tuple-element.36), channel_id=1, replica_groups=mesh['gx'=4,'gy'=8] {'gx','gy'}, dimensions={0} | all-to-all | bytes 163840 | tf_op jit(solution)/shard_map/all_to_all | solution.py:304
  54.9 0.5 step3.1
  55.4 8.9 %all_to_all.35.recv = f32[32,1,1,128]{3,2,1,0:T(1,128)S(1)} all-to-all(f32[32,1,1,128]{3,2,1,0:T(1,128)S(1)} %get-tuple-element.39), channel_id=1, replica_groups=mesh['gx'=4,'gy'=8] {'gx','gy'}, dimensions={0} | all-to-all | bytes 32768 | tf_op jit(solution)/shard_map/all_to_all | solution.py:304
  64.3 0.7 %last.1 = (f32[8,128]{1,0:T(8,128)}, f32[8,128]{1,0:T(8,128)}, f32[4,5]{1,0:T(4,128)}) custom-call(f32[32,1,1,128]{3,2,1,0:T(1,128)S(1)} %all_to_all.35.recv, f32[8,128]{1,0:T(8,128)S(1)} %bitcast.7, f32[8,128]{1,0:T(8,128)S(1)} %get-tuple-element.28.start.refs_0_, f32[8,128]{1,0:T(8,128)S(1)} %get-tuple-element.32.refs_0_, ...), custom_call_target="tpu_custom_call" | custom-call | tf_op jit(solution)/shard_map/last/pallas_call | solution.py:356
  (1 shorter events, 0.0 us)
Async XLA Ops:
  0.6 15.4 %copy-start = (f32[2,4,6,128,128]{4,3,2,1,0:T(8,128)S(1)}, f32[2,4,6,128,128]{4,3,2,1,0:T(8,128)}, u32[]{:S(2)}) copy-start(f32[2,4,6,128,128]{4,3,2,1,0:T(8,128)} %tiles.9) | copy-start | bytes 9437188
  0.6 0.8 %copy-start.1 = (f32[2,4,128]{2,1,0:T(4,128)S(1)}, f32[2,4,128]{2,1,0:T(4,128)}, u32[]{:S(2)}) copy-start(f32[2,4,128]{2,1,0:T(4,128)} %param.9) | copy-start | bytes 12292
  1.5 14.6 %copy-start.2 = (f32[2,4,128]{2,1,0:T(4,128)S(1)}, f32[2,4,128]{2,1,0:T(4,128)}, u32[]{:S(2)}) copy-start(f32[2,4,128]{2,1,0:T(4,128)} %param.9) | copy-start | bytes 12292
  1.5 14.6 %copy-start.3 = (s32[2,4,6]{2,1,0:T(4,128)S(1)}, s32[2,4,6]{2,1,0:T(4,128)}, u32[]{:S(2)}) copy-start(s32[2,4,6]{2,1,0:T(4,128)} %codes.1) | copy-start | bytes 580
  1.5 14.6 %copy-start.4 = (f32[2,4,128]{2,1,0:T(4,128)S(1)}, f32[2,4,128]{2,1,0:T(4,128)}, u32[]{:S(2)}) copy-start(f32[2,4,128]{2,1,0:T(4,128)} %param.8) | copy-start | bytes 12292
  1.5 14.6 %copy-start.5 = (s32[2,4]{1,0:T(2,128)S(1)}, s32[2,4]{1,0:T(2,128)}, u32[]{:S(2)}) copy-start(s32[2,4]{1,0:T(2,128)} %counts.1) | copy-start | bytes 100

commit v7 on v6

--- a/solution.py
+++ b/solution.py
@@ -106,10 +106,11 @@
             term = tiles[x, y, s] * padded[row]
             total = term if total is None else total + term
         column = jnp.sum(total, axis=1, keepdims=True)
-        row = jnp.zeros((8, blk), jnp.float32)
+        halves = [jnp.zeros((8, blk), jnp.float32)] * 2
         for k in range(0, blk, 8):
-            row = jnp.where(eye[k : k + 8], column[k : k + 8], row)
-        out.append(jnp.sum(row, axis=0, keepdims=True))
+            half = (k // 8) % 2
+            halves[half] = jnp.where(eye[k : k + 8], column[k : k + 8], halves[half])
+        out.append(jnp.sum(halves[0] + halves[1], axis=0, keepdims=True))
     return jnp.concatenate(out, axis=0)
 
 

time: 65.3 us -> 65.3 us (level)
  no operation moved by 1% of the time
where the time goes in v7:
time: 65.3 us; the launch traced here: 65 us
  blocking collectives  60.2 us (92%)
  Pallas kernels  3.22 us (5%)
  local copies, waits for them, and re-layouts  0.85 us (1%)
  between operations  0.72 us (1%)
    all_to_all x6, blocking collectives, exchange(): return lax.all_to_all(send, AXES, 0, 0, tiled=True)  60.2 us
    pallas_call x3, Pallas kernels, body(): pl.pallas_call(functools.partial(step_kernel, shape, step), out_shape=(ou...  1.5 us

profile of v7, /device:TPU:0, one launch (start us, length us, event | category | flops | bytes accessed | tf_op | source)
XLA Modules:
  0.0 65.0 jit_solution(17333449396050636897)
XLA Ops:
  0.6 0.0 copy-start
  0.6 0.0 copy-start.1
  0.7 0.8 %copy-done.1 = f32[2,4,128]{2,1,0:T(4,128)S(1)} copy-done((f32[2,4,128]{2,1,0:T(4,128)S(1)}, f32[2,4,128]{2,1,0:T(4,128)}, u32[]{:S(2)}) %copy-start.1) | copy-done | bytes 4120
  1.5 0.0 copy-start.2
  1.5 0.0 copy-start.3
  1.5 0.0 copy-start.4
  1.5 0.0 copy-start.5
  1.5 14.5 %all_to_all.30.recv = f32[32,4,1,128]{3,2,1,0:T(1,128)S(1)} all-to-all(f32[32,4,1,128]{3,2,1,0:T(1,128)S(1)} %first.1), channel_id=1, replica_groups=mesh['gx'=4,'gy'=8] {'gx','gy'}, dimensions={0} | all-to-all | bytes 131072 | tf_op jit(solution)/shard_map/all_to_all | solution.py:305
  16.1 0.0 copy-done
  16.1 0.0 copy-done.2
  16.1 0.0 copy-done.3
  16.1 0.0 copy-done.4
  16.1 0.0 copy-done.5
  16.1 0.5 start.1
  16.6 9.1 %all_to_all.31.recv = f32[32,4,1,128]{3,2,1,0:T(1,128)S(1)} all-to-all(f32[32,4,1,128]{3,2,1,0:T(1,128)S(1)} %get-tuple-element.27), channel_id=1, replica_groups=mesh['gx'=4,'gy'=8] {'gx','gy'}, dimensions={0} | all-to-all | bytes 131072 | tf_op jit(solution)/shard_map/all_to_all | solution.py:305
  25.7 0.4 step0.1
  26.1 9.2 %all_to_all.32.recv = f32[32,5,1,128]{3,2,1,0:T(1,128)S(1)} all-to-all(f32[32,5,1,128]{3,2,1,0:T(1,128)S(1)} %get-tuple-element.29), channel_id=1, replica_groups=mesh['gx'=4,'gy'=8] {'gx','gy'}, dimensions={0} | all-to-all | bytes 163840 | tf_op jit(solution)/shard_map/all_to_all | solution.py:305
  35.4 0.5 step1.1
  35.9 9.2 %all_to_all.33.recv = f32[32,5,1,128]{3,2,1,0:T(1,128)S(1)} all-to-all(f32[32,5,1,128]{3,2,1,0:T(1,128)S(1)} %get-tuple-element.31), channel_id=1, replica_groups=mesh['gx'=4,'gy'=8] {'gx','gy'}, dimensions={0} | all-to-all | bytes 163840 | tf_op jit(solution)/shard_map/all_to_all | solution.py:305
  45.1 0.5 step2.1
  45.6 9.2 %all_to_all.34.recv = f32[32,5,1,128]{3,2,1,0:T(1,128)S(1)} all-to-all(f32[32,5,1,128]{3,2,1,0:T(1,128)S(1)} %get-tuple-element.36), channel_id=1, replica_groups=mesh['gx'=4,'gy'=8] {'gx','gy'}, dimensions={0} | all-to-all | bytes 163840 | tf_op jit(solution)/shard_map/all_to_all | solution.py:305
  54.9 0.5 step3.1
  55.4 8.9 %all_to_all.35.recv = f32[32,1,1,128]{3,2,1,0:T(1,128)S(1)} all-to-all(f32[32,1,1,128]{3,2,1,0:T(1,128)S(1)} %get-tuple-element.39), channel_id=1, replica_groups=mesh['gx'=4,'gy'=8] {'gx','gy'}, dimensions={0} | all-to-all | bytes 32768 | tf_op jit(solution)/shard_map/all_to_all | solution.py:305
  64.3 0.7 %last.1 = (f32[8,128]{1,0:T(8,128)}, f32[8,128]{1,0:T(8,128)}, f32[4,5]{1,0:T(4,128)}) custom-call(f32[32,1,1,128]{3,2,1,0:T(1,128)S(1)} %all_to_all.35.recv, f32[8,128]{1,0:T(8,128)S(1)} %bitcast.7, f32[8,128]{1,0:T(8,128)S(1)} %get-tuple-element.28.start.refs_0_, f32[8,128]{1,0:T(8,128)S(1)} %get-tuple-element.32.refs_0_, ...), custom_call_target="tpu_custom_call" | custom-call | tf_op jit(solution)/shard_map/last/pallas_call | solution.py:357
  (1 shorter events, 0.0 us)
Async XLA Ops:
  0.6 15.4 %copy-start = (f32[2,4,6,128,128]{4,3,2,1,0:T(8,128)S(1)}, f32[2,4,6,128,128]{4,3,2,1,0:T(8,128)}, u32[]{:S(2)}) copy-start(f32[2,4,6,128,128]{4,3,2,1,0:T(8,128)} %tiles.9) | copy-start | bytes 9437188
  0.6 0.8 %copy-start.1 = (f32[2,4,128]{2,1,0:T(4,128)S(1)}, f32[2,4,128]{2,1,0:T(4,128)}, u32[]{:S(2)}) copy-start(f32[2,4,128]{2,1,0:T(4,128)} %param.9) | copy-start | bytes 12292
  1.5 14.6 %copy-start.2 = (f32[2,4,128]{2,1,0:T(4,128)S(1)}, f32[2,4,128]{2,1,0:T(4,128)}, u32[]{:S(2)}) copy-start(f32[2,4,128]{2,1,0:T(4,128)} %param.9) | copy-start | bytes 12292
  1.5 14.6 %copy-start.3 = (s32[2,4,6]{2,1,0:T(4,128)S(1)}, s32[2,4,6]{2,1,0:T(4,128)}, u32[]{:S(2)}) copy-start(s32[2,4,6]{2,1,0:T(4,128)} %codes.1) | copy-start | bytes 580
  1.5 14.6 %copy-start.4 = (f32[2,4,128]{2,1,0:T(4,128)S(1)}, f32[2,4,128]{2,1,0:T(4,128)}, u32[]{:S(2)}) copy-start(f32[2,4,128]{2,1,0:T(4,128)} %param.8) | copy-start | bytes 12292
  1.5 14.6 %copy-start.5 = (s32[2,4]{1,0:T(2,128)S(1)}, s32[2,4]{1,0:T(2,128)}, u32[]{:S(2)}) copy-start(s32[2,4]{1,0:T(2,128)} %counts.1) | copy-start | bytes 100
